TPU v7x, 32 devices: a whole 2x2x4 slice. The times are simulated.
32 devices in a mesh: gx: 2 (over y), gy: 4 (over x, core), gz: 4 (over z).
Axes of the slice: x: 2, y: 2, z: 4, core: 2. Of those that a mesh axis runs over, the one named last changes fastest.
Arguments:
- density: float32 [32, 64, 4096], P('gx', 'gy', 'gz'), may hold values from -19 to 19
Outputs:
- potential: float32 [32, 64, 4096], P('gx', 'gy', 'gz')
- coulomb: float32 [64, 64], replicated
All inputs are finite; a program needn't handle non-finite values.
Results may differ from a plain program's by a relative error of at most 0.000057.
Values sent between devices are 32-bit elements; how exact they have to be, the bound alone decides.
No kernel may reach another device: no remote copies, remote signals or barrier semaphores. Data moves between devices by JAX's collectives and lax.ppermute only.
A program may use at most 64 MiB of HBM per device.

v0:
```python
import jax
import jax.numpy as jnp
from jax import lax
from jax.sharding import PartitionSpec as P

PAIRS = 64
LEVELS = 6
COARSE_SWEEPS = 8
OMEGA = 2.0 / 3.0


def extended_2(x, sides, width):
    for axis, dim in sides:
        size, length = (lax.axis_size(axis), x.shape[dim])
        up = [(i, (i + 1) % size) for i in range(size - 1)]
        down = [(j, i) for i, j in up]
        last = lax.slice_in_dim(x, length - width, length, axis=dim)
        initial = lax.slice_in_dim(x, 0, width, axis=dim)
        before = lax.ppermute(last, axis, up)
        after = lax.ppermute(initial, axis, down)
        x = jnp.concatenate([before, x, after], axis=dim)
    return x


def neighbours(padded):
    total = padded[2:, 1:-1, 1:-1] + padded[:-2, 1:-1, 1:-1]
    total = total + padded[1:-1, 2:, 1:-1] + padded[1:-1, :-2, 1:-1]
    return total + padded[1:-1, 1:-1, 2:] + padded[1:-1, 1:-1, :-2]


def apply_inner(padded, factor):
    return factor * (6.0 * padded[1:-1, 1:-1, 1:-1] - neighbours(padded))


def sweep_inner(padded, source, factor):
    return padded[1:-1, 1:-1, 1:-1] + OMEGA * (source - apply_inner(padded, factor)) / (
        6.0 * factor
    )


def zero_rim(current):
    return jnp.pad(current, ((1, 1), (1, 1), (1, 1), (0, 0)))


def restrict(residual):
    size_x, size_y, size_z, count = residual.shape
    grouped = residual.reshape(size_x // 2, 2, size_y // 2, 2, size_z // 2, 2, count)
    return jnp.mean(grouped, axis=(1, 3, 5))


def prolong(correction):
    return jnp.repeat(jnp.repeat(jnp.repeat(correction, 2, axis=0), 2, axis=1), 2, axis=2)


def global_cycle(source, grid_level):
    factor = 0.25 ** (grid_level - 1)
    current = OMEGA * source / (6.0 * factor)
    if grid_level == LEVELS:
        for repeat_no in range(COARSE_SWEEPS - 1):
            current = sweep_inner(zero_rim(current), source, factor)
        return current
    current = sweep_inner(zero_rim(current), source, factor)
    residual = source - apply_inner(zero_rim(current), factor)
    current = current + prolong(global_cycle(restrict(residual), grid_level + 1))
    for repeat_no in range(2):
        current = sweep_inner(zero_rim(current), source, factor)
    return current


def arrange(stacked, block_shape):
    size_x, size_y, size_z, count = block_shape
    devs_x, devs_y, devs_z = (lax.axis_size("gx"), lax.axis_size("gy"), lax.axis_size("gz"))
    grouped = stacked.reshape(devs_x, devs_y, devs_z, size_x, size_y, size_z, count)
    grouped = grouped.transpose(0, 3, 1, 4, 2, 5, 6)
    return grouped.reshape(devs_x * size_x, devs_y * size_y, devs_z * size_z, count)


def own_block(gathered, block_shape):
    size_x, size_y, size_z, count = block_shape
    starts = (
        lax.axis_index("gx") * size_x,
        lax.axis_index("gy") * size_y,
        lax.axis_index("gz") * size_z,
        jnp.int32(0),
    )
    return lax.dynamic_slice(gathered, starts, block_shape)


def edge_mask(length, where, devices):
    position = jnp.arange(length + 2, dtype=jnp.int32) - 1 + where * length
    return (position >= 0) & (position < length * devices)


def inside_mask(block_shape):
    mask_x = edge_mask(block_shape[0], lax.axis_index("gx"), lax.axis_size("gx"))
    mask_y = edge_mask(block_shape[1], lax.axis_index("gy"), lax.axis_size("gy"))
    mask_z = edge_mask(block_shape[2], lax.axis_index("gz"), lax.axis_size("gz"))
    joined = mask_x[:, None, None] & mask_y[None, :, None] & mask_z[None, None, :]
    return joined[..., None].astype(jnp.float32)


def double_sweep(current, source, factor):
    count = current.shape[3]
    extended = extended_2(
        jnp.concatenate([current, source], axis=3), (("gx", 0), ("gy", 1), ("gz", 2)), 2
    )
    source_wide = extended[1:-1, 1:-1, 1:-1, count:]
    swept = sweep_inner(extended[..., :count], source_wide, factor) * inside_mask(current.shape)
    return swept


def distributed(source, grid_level):
    factor = 0.25 ** (grid_level - 1)
    if grid_level == LEVELS - 1:
        stacked = lax.all_gather(source[None], ("gx", "gy", "gz"), axis=0, tiled=True)
        return own_block(global_cycle(arrange(stacked, source.shape), grid_level), source.shape)
    current = OMEGA * source / (6.0 * factor)
    swept = double_sweep(current, source, factor)
    residual = source - apply_inner(swept, factor)
    current = swept[1:-1, 1:-1, 1:-1]
    current = current + prolong(distributed(restrict(residual), grid_level + 1))
    current = sweep_inner(double_sweep(current, source, factor), source, factor)
    return current


def local(density):
    cells_x, cells_y, merged = density.shape
    cells_z = merged // PAIRS
    cells = density.reshape(cells_x, cells_y, cells_z, PAIRS)
    solved = distributed(cells, 1)
    partial_block = jnp.dot(
        cells.reshape(-1, PAIRS).T,
        solved.reshape(-1, PAIRS),
        precision=lax.Precision.HIGHEST,
        preferred_element_type=jnp.float32,
    )
    summed = lax.psum(partial_block, ("gx", "gy", "gz"))
    total_cells = (
        cells_x
        * cells_y
        * cells_z
        * lax.axis_size("gx")
        * lax.axis_size("gy")
        * lax.axis_size("gz")
    )
    coulomb = summed * (4.0 / total_cells)
    return (solved.reshape(cells_x, cells_y, merged), coulomb)


def solution(mesh):
    return jax.shard_map(
        local,
        mesh=mesh,
        in_specs=(P("gx", "gy", "gz"),),
        out_specs=(P("gx", "gy", "gz"), P()),
        check_vma=False,
    )
```

profile of v0, /device:TPU:14, one launch (start us, length us, event | category | flops | bytes accessed | tf_op | source)
XLA Modules:
  0.0 362.6 jit_solution(3952595412670936373)
XLA Ops:
  6.1 4.6 %collective-permute-start.1 = (f32[2,16,16,128]{3,2,1,0:T(8,128)S(1)}, f32[2,16,16,128]{3,2,1,0:T(8,128)S(1)}, u32[]{:S(2)}, u32[]{:S(2)}) collective-permute-start(f32[2,16,16,128]{3,2,1,0:T(8,128)S(1)} %get-tuple-element.10), channel_id=1, source_target_pairs={{16,0},{17,1},{18,2},{19,3},{20,4},{21,5},{22,6},{23,7},{24,8},{25... | collective-permute-start | bytes 786440 | tf_op jit(solution)/shard_map/ppermute | solution.py:20
  10.7 4.0 %collective-permute-done = f32[2,16,16,128]{3,2,1,0:T(8,128)S(1)} collective-permute-done((f32[2,16,16,128]{3,2,1,0:T(8,128)S(1)}, f32[2,16,16,128]{3,2,1,0:T(8,128)S(1)}, u32[]{:S(2)}, u32[]{:S(2)}) %collective-permute-start) | collective-permute-done | bytes 262176 | tf_op jit(solution)/shard_map/ppermute | solution.py:19
  15.9 2.2 fusion.55
  20.1 3.6 %collective-permute-start.3 = (f32[20,2,16,128]{3,2,1,0:T(8,128)S(1)}, f32[20,2,16,128]{3,2,1,0:T(8,128)S(1)}, u32[]{:S(2)}, u32[]{:S(2)}) collective-permute-start(f32[20,2,16,128]{3,2,1,0:T(8,128)S(1)} %get-tuple-element.19), channel_id=1, source_target_pairs={{4,0},{8,4},{12,8},{5,1},{9,5},{13,9},{6,2},{10,6},{14,10},{7,3},{... | collective-permute-start | bytes 983048 | tf_op jit(solution)/shard_map/ppermute | solution.py:20
  23.9 2.7 collective-permute-done.2
  29.3 3.5 collective-permute-start.4
  32.8 2.4 collective-permute-start.5
  35.4 3.8 %collective-permute-done.4 = f32[20,20,2,128]{3,2,1,0:T(2,128)S(1)} collective-permute-done((f32[20,20,2,128]{3,2,1,0:T(2,128)S(1)}, f32[20,20,2,128]{3,2,1,0:T(2,128)S(1)}, u32[]{:S(2)}, u32[]{:S(2)}) %collective-permute-start.4) | collective-permute-done | bytes 409632 | tf_op jit(solution)/shard_map/ppermute | solution.py:19
  39.2 3.5 collective-permute-done.5
  42.7 3.2 fusion.5
  45.9 8.6 %fusion.23 = f32[18,18,18,64]{3,2,1,0:T(8,128)S(1)} fusion(f32[16,16,16,64]{3,2,1,0:T(8,128)S(1)} %reshape.351, f32[20,20,2,128]{3,2,1,0:T(2,128)S(1)} %collective-permute-done.4, f32[20,2,16,128]{3,2,1,0:T(8,128)S(1)} %collective-permute-done.3, f32[20,2,16,128]{3,2,1,0:T(8,128)S(1)} %collective-permute-done.2, ...), kind=kLoop, calls=%fused_computation.29 | loop fusion | flops 8584704 | bytes 14570272 | tf_op jit(solution)/shard_map/mul | solution.py:108
  54.5 2.6 fusion.63
  57.1 3.0 reduce_sum.52
  62.2 4.5 %collective-permute-start.7 = (f32[2,8,8,128]{3,2,1,0:T(8,128)S(1)}, f32[2,8,8,128]{3,2,1,0:T(8,128)S(1)}, u32[]{:S(2)}, u32[]{:S(2)}) collective-permute-start(f32[2,8,8,128]{3,2,1,0:T(8,128)S(1)} %get-tuple-element.8), channel_id=1, source_target_pairs={{16,0},{17,1},{18,2},{19,3},{20,4},{21,5},{22,6},{23,7},{24,8},{25... | collective-permute-start | bytes 196616 | tf_op jit(solution)/shard_map/ppermute | solution.py:20
  70.7 3.6 %collective-permute-start.9 = (f32[12,2,8,128]{3,2,1,0:T(8,128)S(1)}, f32[12,2,8,128]{3,2,1,0:T(8,128)S(1)}, u32[]{:S(2)}, u32[]{:S(2)}) collective-permute-start(f32[12,2,8,128]{3,2,1,0:T(8,128)S(1)} %get-tuple-element.30), channel_id=1, source_target_pairs={{4,0},{8,4},{12,8},{5,1},{9,5},{13,9},{6,2},{10,6},{14,10},{7,3},{... | collective-permute-start | bytes 294920 | tf_op jit(solution)/shard_map/ppermute | solution.py:20
  76.8 3.5 collective-permute-start.10
  80.3 2.4 collective-permute-start.11
  83.9 3.5 collective-permute-done.11
  91.2 4.7 %collective-permute-start.13 = (f32[2,4,4,128]{3,2,1,0:T(4,128)S(1)}, f32[2,4,4,128]{3,2,1,0:T(4,128)S(1)}, u32[]{:S(2)}, u32[]{:S(2)}) collective-permute-start(f32[2,4,4,128]{3,2,1,0:T(4,128)S(1)} %get-tuple-element.47), channel_id=1, source_target_pairs={{16,0},{17,1},{18,2},{19,3},{20,4},{21,5},{22,6},{23,7},{24,8},{25... | collective-permute-start | bytes 49160 | tf_op jit(solution)/shard_map/ppermute | solution.py:20
  99.2 3.6 %collective-permute-start.15 = (f32[8,2,4,128]{3,2,1,0:T(4,128)S(1)}, f32[8,2,4,128]{3,2,1,0:T(4,128)S(1)}, u32[]{:S(2)}, u32[]{:S(2)}) collective-permute-start(f32[8,2,4,128]{3,2,1,0:T(4,128)S(1)} %get-tuple-element.45), channel_id=1, source_target_pairs={{4,0},{8,4},{12,8},{5,1},{9,5},{13,9},{6,2},{10,6},{14,10},{7,3},{... | collective-permute-start | bytes 98312 | tf_op jit(solution)/shard_map/ppermute | solution.py:20
  106.5 3.9 %collective-permute-start.17 = (f32[8,8,2,128]{3,2,1,0:T(2,128)S(1)}, f32[8,8,2,128]{3,2,1,0:T(2,128)S(1)}, u32[]{:S(2)}, u32[]{:S(2)}) collective-permute-start(f32[8,8,2,128]{3,2,1,0:T(2,128)S(1)} %get-tuple-element.38), channel_id=1, source_target_pairs={{1,0},{2,1},{3,2},{5,4},{6,5},{7,6},{9,8},{10,9},{11,10},{13,12},{... | collective-permute-start | bytes 196616 | tf_op jit(solution)/shard_map/ppermute | solution.py:20
  114.4 4.5 %collective-permute-start.19 = (f32[2,2,2,128]{3,2,1,0:T(2,128)S(1)}, f32[2,2,2,128]{3,2,1,0:T(2,128)S(1)}, u32[]{:S(2)}, u32[]{:S(2)}) collective-permute-start(f32[2,2,2,128]{3,2,1,0:T(2,128)S(1)} %pad_maximum_fusion.46), channel_id=1, source_target_pairs={{16,0},{17,1},{18,2},{19,3},{20,4},{21,5},{22,6},{23,7},{24,8},{25... | collective-permute-start | bytes 12296 | tf_op jit(solution)/shard_map/ppermute | solution.py:20
  122.3 3.6 %collective-permute-start.21 = (f32[6,2,2,128]{3,2,1,0:T(2,128)S(1)}, f32[6,2,2,128]{3,2,1,0:T(2,128)S(1)}, u32[]{:S(2)}, u32[]{:S(2)}) collective-permute-start(f32[6,2,2,128]{3,2,1,0:T(2,128)S(1)} %fusion.281), channel_id=1, source_target_pairs={{4,0},{8,4},{12,8},{5,1},{9,5},{13,9},{6,2},{10,6},{14,10},{7,3},{... | collective-permute-start | bytes 36872 | tf_op jit(solution)/shard_map/ppermute | solution.py:20
  129.9 3.9 %collective-permute-start.23 = (f32[6,6,2,128]{3,2,1,0:T(2,128)}, f32[6,6,2,128]{3,2,1,0:T(2,128)}, u32[]{:S(2)}, u32[]{:S(2)}) collective-permute-start(f32[6,6,2,128]{3,2,1,0:T(2,128)} %fusion.211), channel_id=1, source_target_pairs={{1,0},{2,1},{3,2},{5,4},{6,5},{7,6},{9,8},{10,9},{11,10},{13,12},{... | collective-permute-start | bytes 110600 | tf_op jit(solution)/shard_map/ppermute | solution.py:20
  138.5 42.3 %all-reduce.11 = f32[2048]{0:T(1024)S(1)} all-reduce(f32[2048]{0:T(1024)S(1)} %multiply_dynamic-update-slice_fusion), channel_id=2, replica_groups=mesh['gx'=2,'gy'=4,'gz'=4] {'gx','gy','gz'}, use_global_device_ids=true, to_apply=%add.11 | all-reduce | flops 2048 | bytes 16384
  183.3 4.5 %collective-permute-start.25 = (f32[2,2,2,128]{3,2,1,0:T(2,128)S(1)}, f32[2,2,2,128]{3,2,1,0:T(2,128)S(1)}, u32[]{:S(2)}, u32[]{:S(2)}) collective-permute-start(f32[2,2,2,128]{3,2,1,0:T(2,128)S(1)} %pad_maximum_fusion.47), channel_id=1, source_target_pairs={{16,0},{17,1},{18,2},{19,3},{20,4},{21,5},{22,6},{23,7},{24,8},{25... | collective-permute-start | bytes 12296 | tf_op jit(solution)/shard_map/ppermute | solution.py:20
  191.2 3.6 %collective-permute-start.27 = (f32[6,2,2,128]{3,2,1,0:T(2,128)S(1)}, f32[6,2,2,128]{3,2,1,0:T(2,128)S(1)}, u32[]{:S(2)}, u32[]{:S(2)}) collective-permute-start(f32[6,2,2,128]{3,2,1,0:T(2,128)S(1)} %fusion.283), channel_id=1, source_target_pairs={{4,0},{8,4},{12,8},{5,1},{9,5},{13,9},{6,2},{10,6},{14,10},{7,3},{... | collective-permute-start | bytes 36872 | tf_op jit(solution)/shard_map/ppermute | solution.py:20
  196.3 2.5 collective-permute-start.28
  198.8 3.3 collective-permute-start.29
  202.1 2.6 collective-permute-done.29
  206.4 4.5 %collective-permute-start.31 = (f32[2,4,4,128]{3,2,1,0:T(4,128)S(1)}, f32[2,4,4,128]{3,2,1,0:T(4,128)S(1)}, u32[]{:S(2)}, u32[]{:S(2)}) collective-permute-start(f32[2,4,4,128]{3,2,1,0:T(4,128)S(1)} %get-tuple-element.43), channel_id=1, source_target_pairs={{16,0},{17,1},{18,2},{19,3},{20,4},{21,5},{22,6},{23,7},{24,8},{25... | collective-permute-start | bytes 49160 | tf_op jit(solution)/shard_map/ppermute | solution.py:20
  214.4 3.6 %collective-permute-start.33 = (f32[8,2,4,128]{3,2,1,0:T(4,128)S(1)}, f32[8,2,4,128]{3,2,1,0:T(4,128)S(1)}, u32[]{:S(2)}, u32[]{:S(2)}) collective-permute-start(f32[8,2,4,128]{3,2,1,0:T(4,128)S(1)} %get-tuple-element.41), channel_id=1, source_target_pairs={{4,0},{8,4},{12,8},{5,1},{9,5},{13,9},{6,2},{10,6},{14,10},{7,3},{... | collective-permute-start | bytes 98312 | tf_op jit(solution)/shard_map/ppermute | solution.py:20
  221.7 3.9 %collective-permute-start.35 = (f32[8,8,2,128]{3,2,1,0:T(2,128)S(1)}, f32[8,8,2,128]{3,2,1,0:T(2,128)S(1)}, u32[]{:S(2)}, u32[]{:S(2)}) collective-permute-start(f32[8,8,2,128]{3,2,1,0:T(2,128)S(1)} %get-tuple-element.36), channel_id=1, source_target_pairs={{1,0},{2,1},{3,2},{5,4},{6,5},{7,6},{9,8},{10,9},{11,10},{13,12},{... | collective-permute-start | bytes 196616 | tf_op jit(solution)/shard_map/ppermute | solution.py:20
  230.5 4.5 %collective-permute-start.37 = (f32[2,8,8,128]{3,2,1,0:T(8,128)S(1)}, f32[2,8,8,128]{3,2,1,0:T(8,128)S(1)}, u32[]{:S(2)}, u32[]{:S(2)}) collective-permute-start(f32[2,8,8,128]{3,2,1,0:T(8,128)S(1)} %get-tuple-element.32), channel_id=1, source_target_pairs={{16,0},{17,1},{18,2},{19,3},{20,4},{21,5},{22,6},{23,7},{24,8},{25... | collective-permute-start | bytes 196616 | tf_op jit(solution)/shard_map/ppermute | solution.py:20
  239.1 3.6 %collective-permute-start.39 = (f32[12,2,8,128]{3,2,1,0:T(8,128)S(1)}, f32[12,2,8,128]{3,2,1,0:T(8,128)S(1)}, u32[]{:S(2)}, u32[]{:S(2)}) collective-permute-start(f32[12,2,8,128]{3,2,1,0:T(8,128)S(1)} %get-tuple-element.28), channel_id=1, source_target_pairs={{4,0},{8,4},{12,8},{5,1},{9,5},{13,9},{6,2},{10,6},{14,10},{7,3},{... | collective-permute-start | bytes 294920 | tf_op jit(solution)/shard_map/ppermute | solution.py:20
  247.1 3.9 %collective-permute-start.41 = (f32[12,12,2,128]{3,2,1,0:T(2,128)S(1)}, f32[12,12,2,128]{3,2,1,0:T(2,128)S(1)}, u32[]{:S(2)}, u32[]{:S(2)}) collective-permute-start(f32[12,12,2,128]{3,2,1,0:T(2,128)S(1)} %get-tuple-element.23), channel_id=1, source_target_pairs={{1,0},{2,1},{3,2},{5,4},{6,5},{7,6},{9,8},{10,9},{11,10},{13,12},{... | collective-permute-start | bytes 442376 | tf_op jit(solution)/shard_map/ppermute | solution.py:20
  260.1 4.6 %collective-permute-start.43 = (f32[2,16,16,128]{3,2,1,0:T(8,128)S(1)}, f32[2,16,16,128]{3,2,1,0:T(8,128)S(1)}, u32[]{:S(2)}, u32[]{:S(2)}) collective-permute-start(f32[2,16,16,128]{3,2,1,0:T(8,128)S(1)} %get-tuple-element.21), channel_id=1, source_target_pairs={{16,0},{17,1},{18,2},{19,3},{20,4},{21,5},{22,6},{23,7},{24,8},{25... | collective-permute-start | bytes 786440 | tf_op jit(solution)/shard_map/ppermute | solution.py:20
  264.7 2.4 collective-permute-done.42
  271.2 3.6 %collective-permute-start.45 = (f32[20,2,16,128]{3,2,1,0:T(8,128)S(1)}, f32[20,2,16,128]{3,2,1,0:T(8,128)S(1)}, u32[]{:S(2)}, u32[]{:S(2)}) collective-permute-start(f32[20,2,16,128]{3,2,1,0:T(8,128)S(1)} %get-tuple-element.17), channel_id=1, source_target_pairs={{4,0},{8,4},{12,8},{5,1},{9,5},{13,9},{6,2},{10,6},{14,10},{7,3},{... | collective-permute-start | bytes 983048 | tf_op jit(solution)/shard_map/ppermute | solution.py:20
  274.8 2.8 collective-permute-done.44
  283.2 4.9 %collective-permute-start.47 = (f32[20,20,2,128]{3,2,1,0:T(2,128)}, f32[20,20,2,128]{3,2,1,0:T(2,128)}, u32[]{:S(2)}, u32[]{:S(2)}) collective-permute-start(f32[20,20,2,128]{3,2,1,0:T(2,128)} %get-tuple-element.12), channel_id=1, source_target_pairs={{1,0},{2,1},{3,2},{5,4},{6,5},{7,6},{9,8},{10,9},{11,10},{13,12},{... | collective-permute-start | bytes 1228808 | tf_op jit(solution)/shard_map/ppermute | solution.py:20
  288.1 2.8 reshape_reshape.3
  293.6 4.6 %fusion.11 = f32[20,20,20,128]{3,2,1,0:T(8,128)S(1)} fusion(f32[16,16,16,64]{3,2,1,0:T(8,128)S(1)} %reshape.351, f32[20,20,2,128]{3,2,1,0:T(2,128)} %collective-permute-done.47, f32[20,2,16,128]{3,2,1,0:T(8,128)S(1)} %collective-permute-done.45, f32[2,16,16,128]{3,2,1,0:T(8,128)S(1)} %collective-permute-done.43, f32[16,16,16,64]{3,2,1,0:T(8,128)} %copy-done.4, ...), kind=kLoop, calls=%fused_computation.13 | loop fusion | flops 7168000 | bytes 8192000 | tf_op jit(solution)/shard_map/concatenate | solution.py:21
  298.2 9.5 %fusion.35 = f32[18,18,18,64]{3,2,1,0:T(8,128)S(1)} fusion(f32[16,16,16,64]{3,2,1,0:T(8,128)S(1)} %reshape.351, f32[20,20,2,128]{3,2,1,0:T(2,128)} %collective-permute-done.46, f32[20,2,16,128]{3,2,1,0:T(8,128)S(1)} %collective-permute-done.45, f32[20,2,16,128]{3,2,1,0:T(8,128)S(1)} %collective-permute-done.44, ...), kind=kLoop, calls=%fused_computation.41 | loop fusion | flops 8584704 | bytes 14570272 | tf_op jit(solution)/shard_map/mul | solution.py:108
  307.7 3.1 fusion.61
  310.8 2.9 reshape.365
  313.7 5.2 %convolution_bitcast_fusion = f32[64,64]{0,1:T(8,128)S(1)} fusion(f32[4096,64]{1,0:T(8,128)S(1)} %bitcast.73, f32[4096,64]{1,0:T(8,128)} %reshape_reshape.3), kind=kOutput, calls=%fused_computation.108 | convolution fusion | flops 201326592 | bytes 2113536 | tf_op jit(solution)/shard_map/dot_general | solution.py:131
  318.9 43.0 %psum.7 = f32[64,64]{0,1:T(8,128)S(1)} all-reduce(f32[64,64]{0,1:T(8,128)S(1)} %convolution_bitcast_fusion), channel_id=1, replica_groups=mesh['gx'=2,'gy'=4,'gz'=4] {'gx','gy','gz'}, use_global_device_ids=true, to_apply=%region_6.7 | all-reduce | flops 4096 | bytes 32768 | tf_op jit(solution)/shard_map/psum | solution.py:137
  (211 shorter events, 98.7 us)
Async XLA Ops:
  4.8 9.9 %collective-permute-start = (f32[2,16,16,128]{3,2,1,0:T(8,128)S(1)}, f32[2,16,16,128]{3,2,1,0:T(8,128)S(1)}, u32[]{:S(2)}, u32[]{:S(2)}) collective-permute-start(f32[2,16,16,128]{3,2,1,0:T(8,128)S(1)} %get-tuple-element.22), channel_id=1, source_target_pairs={{0,16},{1,17},{2,18},{3,19},{4,20},{5,21},{6,22},{7,23},{8,24},{9,... | collective-permute-start | bytes 786440 | tf_op jit(solution)/shard_map/ppermute | solution.py:19
  6.1 9.8 %collective-permute-start.1 = (f32[2,16,16,128]{3,2,1,0:T(8,128)S(1)}, f32[2,16,16,128]{3,2,1,0:T(8,128)S(1)}, u32[]{:S(2)}, u32[]{:S(2)}) collective-permute-start(f32[2,16,16,128]{3,2,1,0:T(8,128)S(1)} %get-tuple-element.10), channel_id=1, source_target_pairs={{16,0},{17,1},{18,2},{19,3},{20,4},{21,5},{22,6},{23,7},{24,8},{25... | collective-permute-start | bytes 786440 | tf_op jit(solution)/shard_map/ppermute | solution.py:20
  18.2 8.4 %collective-permute-start.2 = (f32[20,2,16,128]{3,2,1,0:T(8,128)S(1)}, f32[20,2,16,128]{3,2,1,0:T(8,128)S(1)}, u32[]{:S(2)}, u32[]{:S(2)}) collective-permute-start(f32[20,2,16,128]{3,2,1,0:T(8,128)S(1)} %get-tuple-element.18), channel_id=1, source_target_pairs={{0,4},{4,8},{8,12},{1,5},{5,9},{9,13},{2,6},{6,10},{10,14},{3,7},{... | collective-permute-start | bytes 983048 | tf_op jit(solution)/shard_map/ppermute | solution.py:19
  20.1 8.2 %collective-permute-start.3 = (f32[20,2,16,128]{3,2,1,0:T(8,128)S(1)}, f32[20,2,16,128]{3,2,1,0:T(8,128)S(1)}, u32[]{:S(2)}, u32[]{:S(2)}) collective-permute-start(f32[20,2,16,128]{3,2,1,0:T(8,128)S(1)} %get-tuple-element.19), channel_id=1, source_target_pairs={{4,0},{8,4},{12,8},{5,1},{9,5},{13,9},{6,2},{10,6},{14,10},{7,3},{... | collective-permute-start | bytes 983048 | tf_op jit(solution)/shard_map/ppermute | solution.py:20
  29.3 9.8 %collective-permute-start.4 = (f32[20,20,2,128]{3,2,1,0:T(2,128)S(1)}, f32[20,20,2,128]{3,2,1,0:T(2,128)S(1)}, u32[]{:S(2)}, u32[]{:S(2)}) collective-permute-start(f32[20,20,2,128]{3,2,1,0:T(2,128)S(1)} %get-tuple-element.15), channel_id=1, source_target_pairs={{0,1},{1,2},{2,3},{4,5},{5,6},{6,7},{8,9},{9,10},{10,11},{12,13},{... | collective-permute-start | bytes 1228808 | tf_op jit(solution)/shard_map/ppermute | solution.py:19
  32.8 9.8 %collective-permute-start.5 = (f32[20,20,2,128]{3,2,1,0:T(2,128)S(1)}, f32[20,20,2,128]{3,2,1,0:T(2,128)S(1)}, u32[]{:S(2)}, u32[]{:S(2)}) collective-permute-start(f32[20,20,2,128]{3,2,1,0:T(2,128)S(1)} %get-tuple-element.14), channel_id=1, source_target_pairs={{1,0},{2,1},{3,2},{5,4},{6,5},{7,6},{9,8},{10,9},{11,10},{13,12},{... | collective-permute-start | bytes 1228808 | tf_op jit(solution)/shard_map/ppermute | solution.py:20
  60.9 6.6 %collective-permute-start.6 = (f32[2,8,8,128]{3,2,1,0:T(8,128)S(1)}, f32[2,8,8,128]{3,2,1,0:T(8,128)S(1)}, u32[]{:S(2)}, u32[]{:S(2)}) collective-permute-start(f32[2,8,8,128]{3,2,1,0:T(8,128)S(1)} %get-tuple-element.33), channel_id=1, source_target_pairs={{0,16},{1,17},{2,18},{3,19},{4,20},{5,21},{6,22},{7,23},{8,24},{9,... | collective-permute-start | bytes 196616 | tf_op jit(solution)/shard_map/ppermute | solution.py:19
  62.2 6.4 %collective-permute-start.7 = (f32[2,8,8,128]{3,2,1,0:T(8,128)S(1)}, f32[2,8,8,128]{3,2,1,0:T(8,128)S(1)}, u32[]{:S(2)}, u32[]{:S(2)}) collective-permute-start(f32[2,8,8,128]{3,2,1,0:T(8,128)S(1)} %get-tuple-element.8), channel_id=1, source_target_pairs={{16,0},{17,1},{18,2},{19,3},{20,4},{21,5},{22,6},{23,7},{24,8},{25... | collective-permute-start | bytes 196616 | tf_op jit(solution)/shard_map/ppermute | solution.py:20
  68.8 5.9 %collective-permute-start.8 = (f32[12,2,8,128]{3,2,1,0:T(8,128)S(1)}, f32[12,2,8,128]{3,2,1,0:T(8,128)S(1)}, u32[]{:S(2)}, u32[]{:S(2)}) collective-permute-start(f32[12,2,8,128]{3,2,1,0:T(8,128)S(1)} %get-tuple-element.29), channel_id=1, source_target_pairs={{0,4},{4,8},{8,12},{1,5},{5,9},{9,13},{2,6},{6,10},{10,14},{3,7},{... | collective-permute-start | bytes 294920 | tf_op jit(solution)/shard_map/ppermute | solution.py:19
  70.7 5.8 %collective-permute-start.9 = (f32[12,2,8,128]{3,2,1,0:T(8,128)S(1)}, f32[12,2,8,128]{3,2,1,0:T(8,128)S(1)}, u32[]{:S(2)}, u32[]{:S(2)}) collective-permute-start(f32[12,2,8,128]{3,2,1,0:T(8,128)S(1)} %get-tuple-element.30), channel_id=1, source_target_pairs={{4,0},{8,4},{12,8},{5,1},{9,5},{13,9},{6,2},{10,6},{14,10},{7,3},{... | collective-permute-start | bytes 294920 | tf_op jit(solution)/shard_map/ppermute | solution.py:20
  76.8 7.0 %collective-permute-start.10 = (f32[12,12,2,128]{3,2,1,0:T(2,128)S(1)}, f32[12,12,2,128]{3,2,1,0:T(2,128)S(1)}, u32[]{:S(2)}, u32[]{:S(2)}) collective-permute-start(f32[12,12,2,128]{3,2,1,0:T(2,128)S(1)} %get-tuple-element.26), channel_id=1, source_target_pairs={{0,1},{1,2},{2,3},{4,5},{5,6},{6,7},{8,9},{9,10},{10,11},{12,13},{... | collective-permute-start | bytes 442376 | tf_op jit(solution)/shard_map/ppermute | solution.py:19
  80.3 7.0 %collective-permute-start.11 = (f32[12,12,2,128]{3,2,1,0:T(2,128)S(1)}, f32[12,12,2,128]{3,2,1,0:T(2,128)S(1)}, u32[]{:S(2)}, u32[]{:S(2)}) collective-permute-start(f32[12,12,2,128]{3,2,1,0:T(2,128)S(1)} %get-tuple-element.25), channel_id=1, source_target_pairs={{1,0},{2,1},{3,2},{5,4},{6,5},{7,6},{9,8},{10,9},{11,10},{13,12},{... | collective-permute-start | bytes 442376 | tf_op jit(solution)/shard_map/ppermute | solution.py:20
  89.9 6.1 %collective-permute-start.12 = (f32[2,4,4,128]{3,2,1,0:T(4,128)S(1)}, f32[2,4,4,128]{3,2,1,0:T(4,128)S(1)}, u32[]{:S(2)}, u32[]{:S(2)}) collective-permute-start(f32[2,4,4,128]{3,2,1,0:T(4,128)S(1)} %get-tuple-element.46), channel_id=1, source_target_pairs={{0,16},{1,17},{2,18},{3,19},{4,20},{5,21},{6,22},{7,23},{8,24},{9,... | collective-permute-start | bytes 49160 | tf_op jit(solution)/shard_map/ppermute | solution.py:19
  91.2 6.0 %collective-permute-start.13 = (f32[2,4,4,128]{3,2,1,0:T(4,128)S(1)}, f32[2,4,4,128]{3,2,1,0:T(4,128)S(1)}, u32[]{:S(2)}, u32[]{:S(2)}) collective-permute-start(f32[2,4,4,128]{3,2,1,0:T(4,128)S(1)} %get-tuple-element.47), channel_id=1, source_target_pairs={{16,0},{17,1},{18,2},{19,3},{20,4},{21,5},{22,6},{23,7},{24,8},{25... | collective-permute-start | bytes 49160 | tf_op jit(solution)/shard_map/ppermute | solution.py:20
  97.2 5.7 %collective-permute-start.14 = (f32[8,2,4,128]{3,2,1,0:T(4,128)S(1)}, f32[8,2,4,128]{3,2,1,0:T(4,128)S(1)}, u32[]{:S(2)}, u32[]{:S(2)}) collective-permute-start(f32[8,2,4,128]{3,2,1,0:T(4,128)S(1)} %get-tuple-element.44), channel_id=1, source_target_pairs={{0,4},{4,8},{8,12},{1,5},{5,9},{9,13},{2,6},{6,10},{10,14},{3,7},{... | collective-permute-start | bytes 98312 | tf_op jit(solution)/shard_map/ppermute | solution.py:19
  99.2 5.2 %collective-permute-start.15 = (f32[8,2,4,128]{3,2,1,0:T(4,128)S(1)}, f32[8,2,4,128]{3,2,1,0:T(4,128)S(1)}, u32[]{:S(2)}, u32[]{:S(2)}) collective-permute-start(f32[8,2,4,128]{3,2,1,0:T(4,128)S(1)} %get-tuple-element.45), channel_id=1, source_target_pairs={{4,0},{8,4},{12,8},{5,1},{9,5},{13,9},{6,2},{10,6},{14,10},{7,3},{... | collective-permute-start | bytes 98312 | tf_op jit(solution)/shard_map/ppermute | solution.py:20
  104.6 6.4 %collective-permute-start.16 = (f32[8,8,2,128]{3,2,1,0:T(2,128)S(1)}, f32[8,8,2,128]{3,2,1,0:T(2,128)S(1)}, u32[]{:S(2)}, u32[]{:S(2)}) collective-permute-start(f32[8,8,2,128]{3,2,1,0:T(2,128)S(1)} %get-tuple-element.39), channel_id=1, source_target_pairs={{0,1},{1,2},{2,3},{4,5},{5,6},{6,7},{8,9},{9,10},{10,11},{12,13},{... | collective-permute-start | bytes 196616 | tf_op jit(solution)/shard_map/ppermute | solution.py:19
  106.5 6.2 %collective-permute-start.17 = (f32[8,8,2,128]{3,2,1,0:T(2,128)S(1)}, f32[8,8,2,128]{3,2,1,0:T(2,128)S(1)}, u32[]{:S(2)}, u32[]{:S(2)}) collective-permute-start(f32[8,8,2,128]{3,2,1,0:T(2,128)S(1)} %get-tuple-element.38), channel_id=1, source_target_pairs={{1,0},{2,1},{3,2},{5,4},{6,5},{7,6},{9,8},{10,9},{11,10},{13,12},{... | collective-permute-start | bytes 196616 | tf_op jit(solution)/shard_map/ppermute | solution.py:20
  113.1 6.6 %collective-permute-start.18 = (f32[2,2,2,128]{3,2,1,0:T(2,128)S(1)}, f32[2,2,2,128]{3,2,1,0:T(2,128)S(1)}, u32[]{:S(2)}, u32[]{:S(2)}) collective-permute-start(f32[2,2,2,128]{3,2,1,0:T(2,128)S(1)} %pad_maximum_fusion.46), channel_id=1, source_target_pairs={{0,16},{1,17},{2,18},{3,19},{4,20},{5,21},{6,22},{7,23},{8,24},{9,... | collective-permute-start | bytes 12296 | tf_op jit(solution)/shard_map/ppermute | solution.py:19
  114.4 5.9 %collective-permute-start.19 = (f32[2,2,2,128]{3,2,1,0:T(2,128)S(1)}, f32[2,2,2,128]{3,2,1,0:T(2,128)S(1)}, u32[]{:S(2)}, u32[]{:S(2)}) collective-permute-start(f32[2,2,2,128]{3,2,1,0:T(2,128)S(1)} %pad_maximum_fusion.46), channel_id=1, source_target_pairs={{16,0},{17,1},{18,2},{19,3},{20,4},{21,5},{22,6},{23,7},{24,8},{25... | collective-permute-start | bytes 12296 | tf_op jit(solution)/shard_map/ppermute | solution.py:20
  120.3 5.6 %collective-permute-start.20 = (f32[6,2,2,128]{3,2,1,0:T(2,128)S(1)}, f32[6,2,2,128]{3,2,1,0:T(2,128)S(1)}, u32[]{:S(2)}, u32[]{:S(2)}) collective-permute-start(f32[6,2,2,128]{3,2,1,0:T(2,128)S(1)} %fusion.281), channel_id=1, source_target_pairs={{0,4},{4,8},{8,12},{1,5},{5,9},{9,13},{2,6},{6,10},{10,14},{3,7},{... | collective-permute-start | bytes 36872 | tf_op jit(solution)/shard_map/ppermute | solution.py:19
  122.3 5.0 %collective-permute-start.21 = (f32[6,2,2,128]{3,2,1,0:T(2,128)S(1)}, f32[6,2,2,128]{3,2,1,0:T(2,128)S(1)}, u32[]{:S(2)}, u32[]{:S(2)}) collective-permute-start(f32[6,2,2,128]{3,2,1,0:T(2,128)S(1)} %fusion.281), channel_id=1, source_target_pairs={{4,0},{8,4},{12,8},{5,1},{9,5},{13,9},{6,2},{10,6},{14,10},{7,3},{... | collective-permute-start | bytes 36872 | tf_op jit(solution)/shard_map/ppermute | solution.py:20
  128.0 6.0 %collective-permute-start.22 = (f32[6,6,2,128]{3,2,1,0:T(2,128)}, f32[6,6,2,128]{3,2,1,0:T(2,128)S(1)}, u32[]{:S(2)}, u32[]{:S(2)}) collective-permute-start(f32[6,6,2,128]{3,2,1,0:T(2,128)} %fusion.211), channel_id=1, source_target_pairs={{0,1},{1,2},{2,3},{4,5},{5,6},{6,7},{8,9},{9,10},{10,11},{12,13},{... | collective-permute-start | bytes 110600 | tf_op jit(solution)/shard_map/ppermute | solution.py:19
  129.9 6.2 %collective-permute-start.23 = (f32[6,6,2,128]{3,2,1,0:T(2,128)}, f32[6,6,2,128]{3,2,1,0:T(2,128)}, u32[]{:S(2)}, u32[]{:S(2)}) collective-permute-start(f32[6,6,2,128]{3,2,1,0:T(2,128)} %fusion.211), channel_id=1, source_target_pairs={{1,0},{2,1},{3,2},{5,4},{6,5},{7,6},{9,8},{10,9},{11,10},{13,12},{... | collective-permute-start | bytes 110600 | tf_op jit(solution)/shard_map/ppermute | solution.py:20
  182.0 5.8 %collective-permute-start.24 = (f32[2,2,2,128]{3,2,1,0:T(2,128)S(1)}, f32[2,2,2,128]{3,2,1,0:T(2,128)S(1)}, u32[]{:S(2)}, u32[]{:S(2)}) collective-permute-start(f32[2,2,2,128]{3,2,1,0:T(2,128)S(1)} %pad_maximum_fusion.47), channel_id=1, source_target_pairs={{0,16},{1,17},{2,18},{3,19},{4,20},{5,21},{6,22},{7,23},{8,24},{9,... | collective-permute-start | bytes 12296 | tf_op jit(solution)/shard_map/ppermute | solution.py:19
  183.3 5.9 %collective-permute-start.25 = (f32[2,2,2,128]{3,2,1,0:T(2,128)S(1)}, f32[2,2,2,128]{3,2,1,0:T(2,128)S(1)}, u32[]{:S(2)}, u32[]{:S(2)}) collective-permute-start(f32[2,2,2,128]{3,2,1,0:T(2,128)S(1)} %pad_maximum_fusion.47), channel_id=1, source_target_pairs={{16,0},{17,1},{18,2},{19,3},{20,4},{21,5},{22,6},{23,7},{24,8},{25... | collective-permute-start | bytes 12296 | tf_op jit(solution)/shard_map/ppermute | solution.py:20
  189.3 5.6 %collective-permute-start.26 = (f32[6,2,2,128]{3,2,1,0:T(2,128)S(1)}, f32[6,2,2,128]{3,2,1,0:T(2,128)S(1)}, u32[]{:S(2)}, u32[]{:S(2)}) collective-permute-start(f32[6,2,2,128]{3,2,1,0:T(2,128)S(1)} %fusion.283), channel_id=1, source_target_pairs={{0,4},{4,8},{8,12},{1,5},{5,9},{9,13},{2,6},{6,10},{10,14},{3,7},{... | collective-permute-start | bytes 36872 | tf_op jit(solution)/shard_map/ppermute | solution.py:19
  191.2 5.0 %collective-permute-start.27 = (f32[6,2,2,128]{3,2,1,0:T(2,128)S(1)}, f32[6,2,2,128]{3,2,1,0:T(2,128)S(1)}, u32[]{:S(2)}, u32[]{:S(2)}) collective-permute-start(f32[6,2,2,128]{3,2,1,0:T(2,128)S(1)} %fusion.283), channel_id=1, source_target_pairs={{4,0},{8,4},{12,8},{5,1},{9,5},{13,9},{6,2},{10,6},{14,10},{7,3},{... | collective-permute-start | bytes 36872 | tf_op jit(solution)/shard_map/ppermute | solution.py:20
  196.3 5.8 %collective-permute-start.28 = (f32[6,6,2,128]{3,2,1,0:T(2,128)S(1)}, f32[6,6,2,128]{3,2,1,0:T(2,128)S(1)}, u32[]{:S(2)}, u32[]{:S(2)}) collective-permute-start(f32[6,6,2,128]{3,2,1,0:T(2,128)S(1)} %fusion.215), channel_id=1, source_target_pairs={{0,1},{1,2},{2,3},{4,5},{5,6},{6,7},{8,9},{9,10},{10,11},{12,13},{... | collective-permute-start | bytes 110600 | tf_op jit(solution)/shard_map/ppermute | solution.py:19
  198.8 5.9 %collective-permute-start.29 = (f32[6,6,2,128]{3,2,1,0:T(2,128)S(1)}, f32[6,6,2,128]{3,2,1,0:T(2,128)S(1)}, u32[]{:S(2)}, u32[]{:S(2)}) collective-permute-start(f32[6,6,2,128]{3,2,1,0:T(2,128)S(1)} %fusion.215), channel_id=1, source_target_pairs={{1,0},{2,1},{3,2},{5,4},{6,5},{7,6},{9,8},{10,9},{11,10},{13,12},{... | collective-permute-start | bytes 110600 | tf_op jit(solution)/shard_map/ppermute | solution.py:20
  205.1 5.9 %collective-permute-start.30 = (f32[2,4,4,128]{3,2,1,0:T(4,128)S(1)}, f32[2,4,4,128]{3,2,1,0:T(4,128)S(1)}, u32[]{:S(2)}, u32[]{:S(2)}) collective-permute-start(f32[2,4,4,128]{3,2,1,0:T(4,128)S(1)} %get-tuple-element.42), channel_id=1, source_target_pairs={{0,16},{1,17},{2,18},{3,19},{4,20},{5,21},{6,22},{7,23},{8,24},{9,... | collective-permute-start | bytes 49160 | tf_op jit(solution)/shard_map/ppermute | solution.py:19
  206.4 6.0 %collective-permute-start.31 = (f32[2,4,4,128]{3,2,1,0:T(4,128)S(1)}, f32[2,4,4,128]{3,2,1,0:T(4,128)S(1)}, u32[]{:S(2)}, u32[]{:S(2)}) collective-permute-start(f32[2,4,4,128]{3,2,1,0:T(4,128)S(1)} %get-tuple-element.43), channel_id=1, source_target_pairs={{16,0},{17,1},{18,2},{19,3},{20,4},{21,5},{22,6},{23,7},{24,8},{25... | collective-permute-start | bytes 49160 | tf_op jit(solution)/shard_map/ppermute | solution.py:20
  212.5 5.6 %collective-permute-start.32 = (f32[8,2,4,128]{3,2,1,0:T(4,128)S(1)}, f32[8,2,4,128]{3,2,1,0:T(4,128)S(1)}, u32[]{:S(2)}, u32[]{:S(2)}) collective-permute-start(f32[8,2,4,128]{3,2,1,0:T(4,128)S(1)} %get-tuple-element.40), channel_id=1, source_target_pairs={{0,4},{4,8},{8,12},{1,5},{5,9},{9,13},{2,6},{6,10},{10,14},{3,7},{... | collective-permute-start | bytes 98312 | tf_op jit(solution)/shard_map/ppermute | solution.py:19
  214.4 5.2 %collective-permute-start.33 = (f32[8,2,4,128]{3,2,1,0:T(4,128)S(1)}, f32[8,2,4,128]{3,2,1,0:T(4,128)S(1)}, u32[]{:S(2)}, u32[]{:S(2)}) collective-permute-start(f32[8,2,4,128]{3,2,1,0:T(4,128)S(1)} %get-tuple-element.41), channel_id=1, source_target_pairs={{4,0},{8,4},{12,8},{5,1},{9,5},{13,9},{6,2},{10,6},{14,10},{7,3},{... | collective-permute-start | bytes 98312 | tf_op jit(solution)/shard_map/ppermute | solution.py:20
  219.8 6.2 %collective-permute-start.34 = (f32[8,8,2,128]{3,2,1,0:T(2,128)S(1)}, f32[8,8,2,128]{3,2,1,0:T(2,128)S(1)}, u32[]{:S(2)}, u32[]{:S(2)}) collective-permute-start(f32[8,8,2,128]{3,2,1,0:T(2,128)S(1)} %get-tuple-element.37), channel_id=1, source_target_pairs={{0,1},{1,2},{2,3},{4,5},{5,6},{6,7},{8,9},{9,10},{10,11},{12,13},{... | collective-permute-start | bytes 196616 | tf_op jit(solution)/shard_map/ppermute | solution.py:19
  221.7 6.2 %collective-permute-start.35 = (f32[8,8,2,128]{3,2,1,0:T(2,128)S(1)}, f32[8,8,2,128]{3,2,1,0:T(2,128)S(1)}, u32[]{:S(2)}, u32[]{:S(2)}) collective-permute-start(f32[8,8,2,128]{3,2,1,0:T(2,128)S(1)} %get-tuple-element.36), channel_id=1, source_target_pairs={{1,0},{2,1},{3,2},{5,4},{6,5},{7,6},{9,8},{10,9},{11,10},{13,12},{... | collective-permute-start | bytes 196616 | tf_op jit(solution)/shard_map/ppermute | solution.py:20
  229.3 6.2 %collective-permute-start.36 = (f32[2,8,8,128]{3,2,1,0:T(8,128)S(1)}, f32[2,8,8,128]{3,2,1,0:T(8,128)S(1)}, u32[]{:S(2)}, u32[]{:S(2)}) collective-permute-start(f32[2,8,8,128]{3,2,1,0:T(8,128)S(1)} %get-tuple-element.31), channel_id=1, source_target_pairs={{0,16},{1,17},{2,18},{3,19},{4,20},{5,21},{6,22},{7,23},{8,24},{9,... | collective-permute-start | bytes 196616 | tf_op jit(solution)/shard_map/ppermute | solution.py:19
  230.5 6.4 %collective-permute-start.37 = (f32[2,8,8,128]{3,2,1,0:T(8,128)S(1)}, f32[2,8,8,128]{3,2,1,0:T(8,128)S(1)}, u32[]{:S(2)}, u32[]{:S(2)}) collective-permute-start(f32[2,8,8,128]{3,2,1,0:T(8,128)S(1)} %get-tuple-element.32), channel_id=1, source_target_pairs={{16,0},{17,1},{18,2},{19,3},{20,4},{21,5},{22,6},{23,7},{24,8},{25... | collective-permute-start | bytes 196616 | tf_op jit(solution)/shard_map/ppermute | solution.py:20
  237.2 5.9 %collective-permute-start.38 = (f32[12,2,8,128]{3,2,1,0:T(8,128)S(1)}, f32[12,2,8,128]{3,2,1,0:T(8,128)S(1)}, u32[]{:S(2)}, u32[]{:S(2)}) collective-permute-start(f32[12,2,8,128]{3,2,1,0:T(8,128)S(1)} %get-tuple-element.27), channel_id=1, source_target_pairs={{0,4},{4,8},{8,12},{1,5},{5,9},{9,13},{2,6},{6,10},{10,14},{3,7},{... | collective-permute-start | bytes 294920 | tf_op jit(solution)/shard_map/ppermute | solution.py:19
  239.1 5.8 %collective-permute-start.39 = (f32[12,2,8,128]{3,2,1,0:T(8,128)S(1)}, f32[12,2,8,128]{3,2,1,0:T(8,128)S(1)}, u32[]{:S(2)}, u32[]{:S(2)}) collective-permute-start(f32[12,2,8,128]{3,2,1,0:T(8,128)S(1)} %get-tuple-element.28), channel_id=1, source_target_pairs={{4,0},{8,4},{12,8},{5,1},{9,5},{13,9},{6,2},{10,6},{14,10},{7,3},{... | collective-permute-start | bytes 294920 | tf_op jit(solution)/shard_map/ppermute | solution.py:20
  245.2 7.0 %collective-permute-start.40 = (f32[12,12,2,128]{3,2,1,0:T(2,128)S(1)}, f32[12,12,2,128]{3,2,1,0:T(2,128)S(1)}, u32[]{:S(2)}, u32[]{:S(2)}) collective-permute-start(f32[12,12,2,128]{3,2,1,0:T(2,128)S(1)} %get-tuple-element.24), channel_id=1, source_target_pairs={{0,1},{1,2},{2,3},{4,5},{5,6},{6,7},{8,9},{9,10},{10,11},{12,13},{... | collective-permute-start | bytes 442376 | tf_op jit(solution)/shard_map/ppermute | solution.py:19
  247.1 7.0 %collective-permute-start.41 = (f32[12,12,2,128]{3,2,1,0:T(2,128)S(1)}, f32[12,12,2,128]{3,2,1,0:T(2,128)S(1)}, u32[]{:S(2)}, u32[]{:S(2)}) collective-permute-start(f32[12,12,2,128]{3,2,1,0:T(2,128)S(1)} %get-tuple-element.23), channel_id=1, source_target_pairs={{1,0},{2,1},{3,2},{5,4},{6,5},{7,6},{9,8},{10,9},{11,10},{13,12},{... | collective-permute-start | bytes 442376 | tf_op jit(solution)/shard_map/ppermute | solution.py:20
  258.8 8.3 %collective-permute-start.42 = (f32[2,16,16,128]{3,2,1,0:T(8,128)S(1)}, f32[2,16,16,128]{3,2,1,0:T(8,128)S(1)}, u32[]{:S(2)}, u32[]{:S(2)}) collective-permute-start(f32[2,16,16,128]{3,2,1,0:T(8,128)S(1)} %get-tuple-element.20), channel_id=1, source_target_pairs={{0,16},{1,17},{2,18},{3,19},{4,20},{5,21},{6,22},{7,23},{8,24},{9,... | collective-permute-start | bytes 786440 | tf_op jit(solution)/shard_map/ppermute | solution.py:19
  260.1 8.4 %collective-permute-start.43 = (f32[2,16,16,128]{3,2,1,0:T(8,128)S(1)}, f32[2,16,16,128]{3,2,1,0:T(8,128)S(1)}, u32[]{:S(2)}, u32[]{:S(2)}) collective-permute-start(f32[2,16,16,128]{3,2,1,0:T(8,128)S(1)} %get-tuple-element.21), channel_id=1, source_target_pairs={{16,0},{17,1},{18,2},{19,3},{20,4},{21,5},{22,6},{23,7},{24,8},{25... | collective-permute-start | bytes 786440 | tf_op jit(solution)/shard_map/ppermute | solution.py:20
  269.3 8.4 %collective-permute-start.44 = (f32[20,2,16,128]{3,2,1,0:T(8,128)S(1)}, f32[20,2,16,128]{3,2,1,0:T(8,128)S(1)}, u32[]{:S(2)}, u32[]{:S(2)}) collective-permute-start(f32[20,2,16,128]{3,2,1,0:T(8,128)S(1)} %get-tuple-element.16), channel_id=1, source_target_pairs={{0,4},{4,8},{8,12},{1,5},{5,9},{9,13},{2,6},{6,10},{10,14},{3,7},{... | collective-permute-start | bytes 983048 | tf_op jit(solution)/shard_map/ppermute | solution.py:19
  271.2 8.2 %collective-permute-start.45 = (f32[20,2,16,128]{3,2,1,0:T(8,128)S(1)}, f32[20,2,16,128]{3,2,1,0:T(8,128)S(1)}, u32[]{:S(2)}, u32[]{:S(2)}) collective-permute-start(f32[20,2,16,128]{3,2,1,0:T(8,128)S(1)} %get-tuple-element.17), channel_id=1, source_target_pairs={{4,0},{8,4},{12,8},{5,1},{9,5},{13,9},{6,2},{10,6},{14,10},{7,3},{... | collective-permute-start | bytes 983048 | tf_op jit(solution)/shard_map/ppermute | solution.py:20
  281.3 10.2 %collective-permute-start.46 = (f32[20,20,2,128]{3,2,1,0:T(2,128)}, f32[20,20,2,128]{3,2,1,0:T(2,128)}, u32[]{:S(2)}, u32[]{:S(2)}) collective-permute-start(f32[20,20,2,128]{3,2,1,0:T(2,128)} %get-tuple-element.13), channel_id=1, source_target_pairs={{0,1},{1,2},{2,3},{4,5},{5,6},{6,7},{8,9},{9,10},{10,11},{12,13},{... | collective-permute-start | bytes 1228808 | tf_op jit(solution)/shard_map/ppermute | solution.py:19
  283.2 10.5 %collective-permute-start.47 = (f32[20,20,2,128]{3,2,1,0:T(2,128)}, f32[20,20,2,128]{3,2,1,0:T(2,128)}, u32[]{:S(2)}, u32[]{:S(2)}) collective-permute-start(f32[20,20,2,128]{3,2,1,0:T(2,128)} %get-tuple-element.12), channel_id=1, source_target_pairs={{1,0},{2,1},{3,2},{5,4},{6,5},{7,6},{9,8},{10,9},{11,10},{13,12},{... | collective-permute-start | bytes 1228808 | tf_op jit(solution)/shard_map/ppermute | solution.py:20
  (19 other events, 295.5 us)
where the time goes:
time: 365 us; the launch traced here: 363 us
  starting transfers between devices  139 us (38%)
  blocking collectives  85.3 us (23%)
  waiting for transfers between devices  62.1 us (17%)
  other arithmetic  54.9 us (15%)
  local copies, waits for them, and re-layouts  14.3 us (4%)
  matrix products  5.15 us (1%)
    ppermute x24, starting transfers between devices, extended_2(): after = lax.ppermute(initial, axis, down)  94.3 us
    ppermute x24, starting transfers between devices, extended_2(): before = lax.ppermute(last, axis, up)  44.7 us
    psum x1, blocking collectives, local(): summed = lax.psum(partial_block, ('gx', 'gy', 'gz'))  43 us
    unnamed x1, blocking collectives  42.3 us
    ppermute x24, waiting for transfers between devices, extended_2(): after = lax.ppermute(initial, axis, down)  42.2 us
    mul x8, other arithmetic, double_sweep(): sweep_inner(extended[..., :count], source_wide, factor)  23.4 us
    ppermute x24, waiting for transfers between devices, extended_2(): before = lax.ppermute(last, axis, up)  19.9 us
    concatenate x24, other arithmetic, extended_2(): x = jnp.concatenate([before, x, after], axis=dim)  15.6 us
  transfers between devices with their start and end apart: 48, of which 37 were waited for; matrix products, arithmetic and copies ran while one was open for 1% of the time, Pallas kernels for 0%

commit v1 on v0

--- a/solution.py
+++ b/solution.py
@@ -134,7 +134,8 @@
         precision=lax.Precision.HIGHEST,
         preferred_element_type=jnp.float32,
     )
-    summed = lax.psum(partial_block, ("gx", "gy", "gz"))
+    partial = lax.psum(partial_block, ("gy", "gz"))
+    summed = lax.psum(partial, "gx")
     total_cells = (
         cells_x
         * cells_y

time: 365 us -> 391 us (1.071)
  blocking collectives: 85.3 us -> 110 us
    psum x1 -> x2, blocking collectives: 43 us -> 68 us  [the longest x1 58.7 us: local(): partial = lax.psum(partial_block, ('gy', 'gz'))]
where the time goes in v1:
time: 391 us; the launch traced here: 388 us
  starting transfers between devices  139 us (36%)
  blocking collectives  110 us (28%)
  waiting for transfers between devices  62.1 us (16%)
  other arithmetic  54.9 us (14%)
  local copies, waits for them, and re-layouts  14.3 us (4%)
  matrix products  5.15 us (1%)
    ppermute x24, starting transfers between devices, extended_2(): after = lax.ppermute(initial, axis, down)  94.3 us
    psum x1, blocking collectives, local(): partial = lax.psum(partial_block, ('gy', 'gz'))  58.7 us
    ppermute x24, starting transfers between devices, extended_2(): before = lax.ppermute(last, axis, up)  44.7 us
    unnamed x1, blocking collectives  42.3 us
    ppermute x24, waiting for transfers between devices, extended_2(): after = lax.ppermute(initial, axis, down)  42.2 us
    mul x8, other arithmetic, double_sweep(): sweep_inner(extended[..., :count], source_wide, factor)  23.4 us
    ppermute x24, waiting for transfers between devices, extended_2(): before = lax.ppermute(last, axis, up)  19.9 us
    concatenate x24, other arithmetic, extended_2(): x = jnp.concatenate([before, x, after], axis=dim)  15.6 us
  transfers between devices with their start and end apart: 48, of which 37 were waited for; matrix products, arithmetic and copies ran while one was open for 1% of the time, Pallas kernels for 0%

profile of v1, /device:TPU:14, one launch (start us, length us, event | category | flops | bytes accessed | tf_op | source)
XLA Modules:
  0.0 387.6 jit_solution(13496438437662713241)
XLA Ops:
  6.1 4.6 %collective-permute-start.1 = (f32[2,16,16,128]{3,2,1,0:T(8,128)S(1)}, f32[2,16,16,128]{3,2,1,0:T(8,128)S(1)}, u32[]{:S(2)}, u32[]{:S(2)}) collective-permute-start(f32[2,16,16,128]{3,2,1,0:T(8,128)S(1)} %get-tuple-element.10), channel_id=1, source_target_pairs={{16,0},{17,1},{18,2},{19,3},{20,4},{21,5},{22,6},{23,7},{24,8},{25... | collective-permute-start | bytes 786440 | tf_op jit(solution)/shard_map/ppermute | solution.py:20
  10.7 4.0 %collective-permute-done = f32[2,16,16,128]{3,2,1,0:T(8,128)S(1)} collective-permute-done((f32[2,16,16,128]{3,2,1,0:T(8,128)S(1)}, f32[2,16,16,128]{3,2,1,0:T(8,128)S(1)}, u32[]{:S(2)}, u32[]{:S(2)}) %collective-permute-start) | collective-permute-done | bytes 262176 | tf_op jit(solution)/shard_map/ppermute | solution.py:19
  20.1 3.6 collective-permute-start.3
  23.8 2.7 collective-permute-done.2
  29.3 3.5 collective-permute-start.4
  32.8 2.4 collective-permute-start.5
  35.4 3.8 collective-permute-done.4
  39.2 3.5 collective-permute-done.5
  42.6 3.2 fusion.5
  45.9 8.6 %fusion.23 = f32[18,18,18,64]{3,2,1,0:T(8,128)S(1)} fusion(f32[16,16,16,64]{3,2,1,0:T(8,128)S(1)} %reshape.351, f32[20,20,2,128]{3,2,1,0:T(2,128)S(1)} %collective-permute-done.4, f32[20,2,16,128]{3,2,1,0:T(8,128)S(1)} %collective-permute-done.3, f32[20,2,16,128]{3,2,1,0:T(8,128)S(1)} %collective-permute-done.2, ...), kind=kLoop, calls=%fused_computation.29 | loop fusion | flops 8584704 | bytes 14570272 | tf_op jit(solution)/shard_map/mul | solution.py:108
  54.5 2.6 fusion.63
  57.1 3.0 reduce_sum.52
  62.2 4.5 %collective-permute-start.7 = (f32[2,8,8,128]{3,2,1,0:T(8,128)S(1)}, f32[2,8,8,128]{3,2,1,0:T(8,128)S(1)}, u32[]{:S(2)}, u32[]{:S(2)}) collective-permute-start(f32[2,8,8,128]{3,2,1,0:T(8,128)S(1)} %get-tuple-element.8), channel_id=1, source_target_pairs={{16,0},{17,1},{18,2},{19,3},{20,4},{21,5},{22,6},{23,7},{24,8},{25... | collective-permute-start | bytes 196616 | tf_op jit(solution)/shard_map/ppermute | solution.py:20
  70.7 3.6 collective-permute-start.9
  76.8 3.5 collective-permute-start.10
  80.3 2.4 collective-permute-start.11
  83.9 3.5 collective-permute-done.11
  91.2 4.7 %collective-permute-start.13 = (f32[2,4,4,128]{3,2,1,0:T(4,128)S(1)}, f32[2,4,4,128]{3,2,1,0:T(4,128)S(1)}, u32[]{:S(2)}, u32[]{:S(2)}) collective-permute-start(f32[2,4,4,128]{3,2,1,0:T(4,128)S(1)} %get-tuple-element.47), channel_id=1, source_target_pairs={{16,0},{17,1},{18,2},{19,3},{20,4},{21,5},{22,6},{23,7},{24,8},{25... | collective-permute-start | bytes 49160 | tf_op jit(solution)/shard_map/ppermute | solution.py:20
  99.2 3.6 collective-permute-start.15
  106.5 3.9 %collective-permute-start.17 = (f32[8,8,2,128]{3,2,1,0:T(2,128)S(1)}, f32[8,8,2,128]{3,2,1,0:T(2,128)S(1)}, u32[]{:S(2)}, u32[]{:S(2)}) collective-permute-start(f32[8,8,2,128]{3,2,1,0:T(2,128)S(1)} %get-tuple-element.38), channel_id=1, source_target_pairs={{1,0},{2,1},{3,2},{5,4},{6,5},{7,6},{9,8},{10,9},{11,10},{13,12},{... | collective-permute-start | bytes 196616 | tf_op jit(solution)/shard_map/ppermute | solution.py:20
  114.4 4.5 %collective-permute-start.19 = (f32[2,2,2,128]{3,2,1,0:T(2,128)S(1)}, f32[2,2,2,128]{3,2,1,0:T(2,128)S(1)}, u32[]{:S(2)}, u32[]{:S(2)}) collective-permute-start(f32[2,2,2,128]{3,2,1,0:T(2,128)S(1)} %pad_maximum_fusion.46), channel_id=1, source_target_pairs={{16,0},{17,1},{18,2},{19,3},{20,4},{21,5},{22,6},{23,7},{24,8},{25... | collective-permute-start | bytes 12296 | tf_op jit(solution)/shard_map/ppermute | solution.py:20
  122.3 3.6 collective-permute-start.21
  129.9 3.9 %collective-permute-start.23 = (f32[6,6,2,128]{3,2,1,0:T(2,128)}, f32[6,6,2,128]{3,2,1,0:T(2,128)}, u32[]{:S(2)}, u32[]{:S(2)}) collective-permute-start(f32[6,6,2,128]{3,2,1,0:T(2,128)} %fusion.211), channel_id=1, source_target_pairs={{1,0},{2,1},{3,2},{5,4},{6,5},{7,6},{9,8},{10,9},{11,10},{13,12},{... | collective-permute-start | bytes 110600 | tf_op jit(solution)/shard_map/ppermute | solution.py:20
  138.5 42.3 %all-reduce.11 = f32[2048]{0:T(1024)S(1)} all-reduce(f32[2048]{0:T(1024)S(1)} %multiply_dynamic-update-slice_fusion), channel_id=2, replica_groups=mesh['gx'=2,'gy'=4,'gz'=4] {'gx','gy','gz'}, use_global_device_ids=true, to_apply=%add.11 | all-reduce | flops 2048 | bytes 16384
  183.3 4.5 %collective-permute-start.25 = (f32[2,2,2,128]{3,2,1,0:T(2,128)S(1)}, f32[2,2,2,128]{3,2,1,0:T(2,128)S(1)}, u32[]{:S(2)}, u32[]{:S(2)}) collective-permute-start(f32[2,2,2,128]{3,2,1,0:T(2,128)S(1)} %pad_maximum_fusion.47), channel_id=1, source_target_pairs={{16,0},{17,1},{18,2},{19,3},{20,4},{21,5},{22,6},{23,7},{24,8},{25... | collective-permute-start | bytes 12296 | tf_op jit(solution)/shard_map/ppermute | solution.py:20
  191.2 3.6 collective-permute-start.27
  196.3 2.5 collective-permute-start.28
  198.8 3.3 collective-permute-start.29
  202.1 2.6 collective-permute-done.29
  206.4 4.5 %collective-permute-start.31 = (f32[2,4,4,128]{3,2,1,0:T(4,128)S(1)}, f32[2,4,4,128]{3,2,1,0:T(4,128)S(1)}, u32[]{:S(2)}, u32[]{:S(2)}) collective-permute-start(f32[2,4,4,128]{3,2,1,0:T(4,128)S(1)} %get-tuple-element.43), channel_id=1, source_target_pairs={{16,0},{17,1},{18,2},{19,3},{20,4},{21,5},{22,6},{23,7},{24,8},{25... | collective-permute-start | bytes 49160 | tf_op jit(solution)/shard_map/ppermute | solution.py:20
  214.4 3.6 collective-permute-start.33
  221.7 3.9 %collective-permute-start.35 = (f32[8,8,2,128]{3,2,1,0:T(2,128)S(1)}, f32[8,8,2,128]{3,2,1,0:T(2,128)S(1)}, u32[]{:S(2)}, u32[]{:S(2)}) collective-permute-start(f32[8,8,2,128]{3,2,1,0:T(2,128)S(1)} %get-tuple-element.36), channel_id=1, source_target_pairs={{1,0},{2,1},{3,2},{5,4},{6,5},{7,6},{9,8},{10,9},{11,10},{13,12},{... | collective-permute-start | bytes 196616 | tf_op jit(solution)/shard_map/ppermute | solution.py:20
  230.5 4.5 %collective-permute-start.37 = (f32[2,8,8,128]{3,2,1,0:T(8,128)S(1)}, f32[2,8,8,128]{3,2,1,0:T(8,128)S(1)}, u32[]{:S(2)}, u32[]{:S(2)}) collective-permute-start(f32[2,8,8,128]{3,2,1,0:T(8,128)S(1)} %get-tuple-element.32), channel_id=1, source_target_pairs={{16,0},{17,1},{18,2},{19,3},{20,4},{21,5},{22,6},{23,7},{24,8},{25... | collective-permute-start | bytes 196616 | tf_op jit(solution)/shard_map/ppermute | solution.py:20
  239.1 3.6 collective-permute-start.39
  247.1 3.9 %collective-permute-start.41 = (f32[12,12,2,128]{3,2,1,0:T(2,128)S(1)}, f32[12,12,2,128]{3,2,1,0:T(2,128)S(1)}, u32[]{:S(2)}, u32[]{:S(2)}) collective-permute-start(f32[12,12,2,128]{3,2,1,0:T(2,128)S(1)} %get-tuple-element.23), channel_id=1, source_target_pairs={{1,0},{2,1},{3,2},{5,4},{6,5},{7,6},{9,8},{10,9},{11,10},{13,12},{... | collective-permute-start | bytes 442376 | tf_op jit(solution)/shard_map/ppermute | solution.py:20
  260.1 4.6 %collective-permute-start.43 = (f32[2,16,16,128]{3,2,1,0:T(8,128)S(1)}, f32[2,16,16,128]{3,2,1,0:T(8,128)S(1)}, u32[]{:S(2)}, u32[]{:S(2)}) collective-permute-start(f32[2,16,16,128]{3,2,1,0:T(8,128)S(1)} %get-tuple-element.21), channel_id=1, source_target_pairs={{16,0},{17,1},{18,2},{19,3},{20,4},{21,5},{22,6},{23,7},{24,8},{25... | collective-permute-start | bytes 786440 | tf_op jit(solution)/shard_map/ppermute | solution.py:20
  264.7 2.4 collective-permute-done.42
  271.2 3.6 collective-permute-start.45
  274.8 2.8 collective-permute-done.44
  283.2 4.9 %collective-permute-start.47 = (f32[20,20,2,128]{3,2,1,0:T(2,128)}, f32[20,20,2,128]{3,2,1,0:T(2,128)}, u32[]{:S(2)}, u32[]{:S(2)}) collective-permute-start(f32[20,20,2,128]{3,2,1,0:T(2,128)} %get-tuple-element.12), channel_id=1, source_target_pairs={{1,0},{2,1},{3,2},{5,4},{6,5},{7,6},{9,8},{10,9},{11,10},{13,12},{... | collective-permute-start | bytes 1228808 | tf_op jit(solution)/shard_map/ppermute | solution.py:20
  288.1 2.8 reshape_reshape.3
  293.6 4.6 %fusion.11 = f32[20,20,20,128]{3,2,1,0:T(8,128)S(1)} fusion(f32[16,16,16,64]{3,2,1,0:T(8,128)S(1)} %reshape.351, f32[20,20,2,128]{3,2,1,0:T(2,128)} %collective-permute-done.47, f32[20,2,16,128]{3,2,1,0:T(8,128)S(1)} %collective-permute-done.45, f32[2,16,16,128]{3,2,1,0:T(8,128)S(1)} %collective-permute-done.43, f32[16,16,16,64]{3,2,1,0:T(8,128)} %copy-done.4, ...), kind=kLoop, calls=%fused_computation.13 | loop fusion | flops 7168000 | bytes 8192000 | tf_op jit(solution)/shard_map/concatenate | solution.py:21
  298.2 9.5 %fusion.35 = f32[18,18,18,64]{3,2,1,0:T(8,128)S(1)} fusion(f32[16,16,16,64]{3,2,1,0:T(8,128)S(1)} %reshape.351, f32[20,20,2,128]{3,2,1,0:T(2,128)} %collective-permute-done.46, f32[20,2,16,128]{3,2,1,0:T(8,128)S(1)} %collective-permute-done.45, f32[20,2,16,128]{3,2,1,0:T(8,128)S(1)} %collective-permute-done.44, ...), kind=kLoop, calls=%fused_computation.41 | loop fusion | flops 8584704 | bytes 14570272 | tf_op jit(solution)/shard_map/mul | solution.py:108
  307.7 3.1 fusion.61
  310.8 2.9 reshape.365
  313.7 5.2 %convolution_bitcast_fusion = f32[64,64]{0,1:T(8,128)S(1)} fusion(f32[4096,64]{1,0:T(8,128)S(1)} %bitcast.73, f32[4096,64]{1,0:T(8,128)} %reshape_reshape.3), kind=kOutput, calls=%fused_computation.108 | convolution fusion | flops 201326592 | bytes 2113536 | tf_op jit(solution)/shard_map/dot_general | solution.py:131
  318.9 58.7 %psum.14 = f32[64,64]{0,1:T(8,128)S(1)} all-reduce(f32[64,64]{0,1:T(8,128)S(1)} %convolution_bitcast_fusion), channel_id=1, replica_groups=mesh['gx'=2,'gy'=4,'gz'=4] {'gy','gz'}, use_global_device_ids=true, to_apply=%region_6.7 | all-reduce | flops 4096 | bytes 32768 | tf_op jit(solution)/shard_map/psum | solution.py:137
  377.5 9.3 %psum.15 = f32[64,64]{0,1:T(8,128)S(1)} all-reduce(f32[64,64]{0,1:T(8,128)S(1)} %psum.14), channel_id=1, replica_groups=mesh['gx'=2,'gy'=4,'gz'=4] {'gx'}, use_global_device_ids=true, to_apply=%region_7.8 | all-reduce | flops 4096 | bytes 32768 | tf_op jit(solution)/shard_map/psum | solution.py:138
  (212 shorter events, 101.0 us)
Async XLA Ops:
  4.8 9.9 %collective-permute-start = (f32[2,16,16,128]{3,2,1,0:T(8,128)S(1)}, f32[2,16,16,128]{3,2,1,0:T(8,128)S(1)}, u32[]{:S(2)}, u32[]{:S(2)}) collective-permute-start(f32[2,16,16,128]{3,2,1,0:T(8,128)S(1)} %get-tuple-element.22), channel_id=1, source_target_pairs={{0,16},{1,17},{2,18},{3,19},{4,20},{5,21},{6,22},{7,23},{8,24},{9,... | collective-permute-start | bytes 786440 | tf_op jit(solution)/shard_map/ppermute | solution.py:19
  6.1 9.8 %collective-permute-start.1 = (f32[2,16,16,128]{3,2,1,0:T(8,128)S(1)}, f32[2,16,16,128]{3,2,1,0:T(8,128)S(1)}, u32[]{:S(2)}, u32[]{:S(2)}) collective-permute-start(f32[2,16,16,128]{3,2,1,0:T(8,128)S(1)} %get-tuple-element.10), channel_id=1, source_target_pairs={{16,0},{17,1},{18,2},{19,3},{20,4},{21,5},{22,6},{23,7},{24,8},{25... | collective-permute-start | bytes 786440 | tf_op jit(solution)/shard_map/ppermute | solution.py:20
  18.2 8.4 %collective-permute-start.2 = (f32[20,2,16,128]{3,2,1,0:T(8,128)S(1)}, f32[20,2,16,128]{3,2,1,0:T(8,128)S(1)}, u32[]{:S(2)}, u32[]{:S(2)}) collective-permute-start(f32[20,2,16,128]{3,2,1,0:T(8,128)S(1)} %get-tuple-element.18), channel_id=1, source_target_pairs={{0,4},{4,8},{8,12},{1,5},{5,9},{9,13},{2,6},{6,10},{10,14},{3,7},{... | collective-permute-start | bytes 983048 | tf_op jit(solution)/shard_map/ppermute | solution.py:19
  20.1 8.2 %collective-permute-start.3 = (f32[20,2,16,128]{3,2,1,0:T(8,128)S(1)}, f32[20,2,16,128]{3,2,1,0:T(8,128)S(1)}, u32[]{:S(2)}, u32[]{:S(2)}) collective-permute-start(f32[20,2,16,128]{3,2,1,0:T(8,128)S(1)} %get-tuple-element.19), channel_id=1, source_target_pairs={{4,0},{8,4},{12,8},{5,1},{9,5},{13,9},{6,2},{10,6},{14,10},{7,3},{... | collective-permute-start | bytes 983048 | tf_op jit(solution)/shard_map/ppermute | solution.py:20
  29.3 9.8 %collective-permute-start.4 = (f32[20,20,2,128]{3,2,1,0:T(2,128)S(1)}, f32[20,20,2,128]{3,2,1,0:T(2,128)S(1)}, u32[]{:S(2)}, u32[]{:S(2)}) collective-permute-start(f32[20,20,2,128]{3,2,1,0:T(2,128)S(1)} %get-tuple-element.15), channel_id=1, source_target_pairs={{0,1},{1,2},{2,3},{4,5},{5,6},{6,7},{8,9},{9,10},{10,11},{12,13},{... | collective-permute-start | bytes 1228808 | tf_op jit(solution)/shard_map/ppermute | solution.py:19
  32.8 9.8 %collective-permute-start.5 = (f32[20,20,2,128]{3,2,1,0:T(2,128)S(1)}, f32[20,20,2,128]{3,2,1,0:T(2,128)S(1)}, u32[]{:S(2)}, u32[]{:S(2)}) collective-permute-start(f32[20,20,2,128]{3,2,1,0:T(2,128)S(1)} %get-tuple-element.14), channel_id=1, source_target_pairs={{1,0},{2,1},{3,2},{5,4},{6,5},{7,6},{9,8},{10,9},{11,10},{13,12},{... | collective-permute-start | bytes 1228808 | tf_op jit(solution)/shard_map/ppermute | solution.py:20
  60.9 6.6 %collective-permute-start.6 = (f32[2,8,8,128]{3,2,1,0:T(8,128)S(1)}, f32[2,8,8,128]{3,2,1,0:T(8,128)S(1)}, u32[]{:S(2)}, u32[]{:S(2)}) collective-permute-start(f32[2,8,8,128]{3,2,1,0:T(8,128)S(1)} %get-tuple-element.33), channel_id=1, source_target_pairs={{0,16},{1,17},{2,18},{3,19},{4,20},{5,21},{6,22},{7,23},{8,24},{9,... | collective-permute-start | bytes 196616 | tf_op jit(solution)/shard_map/ppermute | solution.py:19
  62.2 6.4 %collective-permute-start.7 = (f32[2,8,8,128]{3,2,1,0:T(8,128)S(1)}, f32[2,8,8,128]{3,2,1,0:T(8,128)S(1)}, u32[]{:S(2)}, u32[]{:S(2)}) collective-permute-start(f32[2,8,8,128]{3,2,1,0:T(8,128)S(1)} %get-tuple-element.8), channel_id=1, source_target_pairs={{16,0},{17,1},{18,2},{19,3},{20,4},{21,5},{22,6},{23,7},{24,8},{25... | collective-permute-start | bytes 196616 | tf_op jit(solution)/shard_map/ppermute | solution.py:20
  68.8 5.9 %collective-permute-start.8 = (f32[12,2,8,128]{3,2,1,0:T(8,128)S(1)}, f32[12,2,8,128]{3,2,1,0:T(8,128)S(1)}, u32[]{:S(2)}, u32[]{:S(2)}) collective-permute-start(f32[12,2,8,128]{3,2,1,0:T(8,128)S(1)} %get-tuple-element.29), channel_id=1, source_target_pairs={{0,4},{4,8},{8,12},{1,5},{5,9},{9,13},{2,6},{6,10},{10,14},{3,7},{... | collective-permute-start | bytes 294920 | tf_op jit(solution)/shard_map/ppermute | solution.py:19
  70.7 5.8 %collective-permute-start.9 = (f32[12,2,8,128]{3,2,1,0:T(8,128)S(1)}, f32[12,2,8,128]{3,2,1,0:T(8,128)S(1)}, u32[]{:S(2)}, u32[]{:S(2)}) collective-permute-start(f32[12,2,8,128]{3,2,1,0:T(8,128)S(1)} %get-tuple-element.30), channel_id=1, source_target_pairs={{4,0},{8,4},{12,8},{5,1},{9,5},{13,9},{6,2},{10,6},{14,10},{7,3},{... | collective-permute-start | bytes 294920 | tf_op jit(solution)/shard_map/ppermute | solution.py:20
  76.8 7.0 %collective-permute-start.10 = (f32[12,12,2,128]{3,2,1,0:T(2,128)S(1)}, f32[12,12,2,128]{3,2,1,0:T(2,128)S(1)}, u32[]{:S(2)}, u32[]{:S(2)}) collective-permute-start(f32[12,12,2,128]{3,2,1,0:T(2,128)S(1)} %get-tuple-element.26), channel_id=1, source_target_pairs={{0,1},{1,2},{2,3},{4,5},{5,6},{6,7},{8,9},{9,10},{10,11},{12,13},{... | collective-permute-start | bytes 442376 | tf_op jit(solution)/shard_map/ppermute | solution.py:19
  80.3 7.0 %collective-permute-start.11 = (f32[12,12,2,128]{3,2,1,0:T(2,128)S(1)}, f32[12,12,2,128]{3,2,1,0:T(2,128)S(1)}, u32[]{:S(2)}, u32[]{:S(2)}) collective-permute-start(f32[12,12,2,128]{3,2,1,0:T(2,128)S(1)} %get-tuple-element.25), channel_id=1, source_target_pairs={{1,0},{2,1},{3,2},{5,4},{6,5},{7,6},{9,8},{10,9},{11,10},{13,12},{... | collective-permute-start | bytes 442376 | tf_op jit(solution)/shard_map/ppermute | solution.py:20
  89.9 6.1 %collective-permute-start.12 = (f32[2,4,4,128]{3,2,1,0:T(4,128)S(1)}, f32[2,4,4,128]{3,2,1,0:T(4,128)S(1)}, u32[]{:S(2)}, u32[]{:S(2)}) collective-permute-start(f32[2,4,4,128]{3,2,1,0:T(4,128)S(1)} %get-tuple-element.46), channel_id=1, source_target_pairs={{0,16},{1,17},{2,18},{3,19},{4,20},{5,21},{6,22},{7,23},{8,24},{9,... | collective-permute-start | bytes 49160 | tf_op jit(solution)/shard_map/ppermute | solution.py:19
  91.2 6.0 %collective-permute-start.13 = (f32[2,4,4,128]{3,2,1,0:T(4,128)S(1)}, f32[2,4,4,128]{3,2,1,0:T(4,128)S(1)}, u32[]{:S(2)}, u32[]{:S(2)}) collective-permute-start(f32[2,4,4,128]{3,2,1,0:T(4,128)S(1)} %get-tuple-element.47), channel_id=1, source_target_pairs={{16,0},{17,1},{18,2},{19,3},{20,4},{21,5},{22,6},{23,7},{24,8},{25... | collective-permute-start | bytes 49160 | tf_op jit(solution)/shard_map/ppermute | solution.py:20
  97.2 5.7 %collective-permute-start.14 = (f32[8,2,4,128]{3,2,1,0:T(4,128)S(1)}, f32[8,2,4,128]{3,2,1,0:T(4,128)S(1)}, u32[]{:S(2)}, u32[]{:S(2)}) collective-permute-start(f32[8,2,4,128]{3,2,1,0:T(4,128)S(1)} %get-tuple-element.44), channel_id=1, source_target_pairs={{0,4},{4,8},{8,12},{1,5},{5,9},{9,13},{2,6},{6,10},{10,14},{3,7},{... | collective-permute-start | bytes 98312 | tf_op jit(solution)/shard_map/ppermute | solution.py:19
  99.2 5.2 %collective-permute-start.15 = (f32[8,2,4,128]{3,2,1,0:T(4,128)S(1)}, f32[8,2,4,128]{3,2,1,0:T(4,128)S(1)}, u32[]{:S(2)}, u32[]{:S(2)}) collective-permute-start(f32[8,2,4,128]{3,2,1,0:T(4,128)S(1)} %get-tuple-element.45), channel_id=1, source_target_pairs={{4,0},{8,4},{12,8},{5,1},{9,5},{13,9},{6,2},{10,6},{14,10},{7,3},{... | collective-permute-start | bytes 98312 | tf_op jit(solution)/shard_map/ppermute | solution.py:20
  104.6 6.4 %collective-permute-start.16 = (f32[8,8,2,128]{3,2,1,0:T(2,128)S(1)}, f32[8,8,2,128]{3,2,1,0:T(2,128)S(1)}, u32[]{:S(2)}, u32[]{:S(2)}) collective-permute-start(f32[8,8,2,128]{3,2,1,0:T(2,128)S(1)} %get-tuple-element.39), channel_id=1, source_target_pairs={{0,1},{1,2},{2,3},{4,5},{5,6},{6,7},{8,9},{9,10},{10,11},{12,13},{... | collective-permute-start | bytes 196616 | tf_op jit(solution)/shard_map/ppermute | solution.py:19
  106.5 6.2 %collective-permute-start.17 = (f32[8,8,2,128]{3,2,1,0:T(2,128)S(1)}, f32[8,8,2,128]{3,2,1,0:T(2,128)S(1)}, u32[]{:S(2)}, u32[]{:S(2)}) collective-permute-start(f32[8,8,2,128]{3,2,1,0:T(2,128)S(1)} %get-tuple-element.38), channel_id=1, source_target_pairs={{1,0},{2,1},{3,2},{5,4},{6,5},{7,6},{9,8},{10,9},{11,10},{13,12},{... | collective-permute-start | bytes 196616 | tf_op jit(solution)/shard_map/ppermute | solution.py:20
  113.1 6.6 %collective-permute-start.18 = (f32[2,2,2,128]{3,2,1,0:T(2,128)S(1)}, f32[2,2,2,128]{3,2,1,0:T(2,128)S(1)}, u32[]{:S(2)}, u32[]{:S(2)}) collective-permute-start(f32[2,2,2,128]{3,2,1,0:T(2,128)S(1)} %pad_maximum_fusion.46), channel_id=1, source_target_pairs={{0,16},{1,17},{2,18},{3,19},{4,20},{5,21},{6,22},{7,23},{8,24},{9,... | collective-permute-start | bytes 12296 | tf_op jit(solution)/shard_map/ppermute | solution.py:19
  114.4 5.9 %collective-permute-start.19 = (f32[2,2,2,128]{3,2,1,0:T(2,128)S(1)}, f32[2,2,2,128]{3,2,1,0:T(2,128)S(1)}, u32[]{:S(2)}, u32[]{:S(2)}) collective-permute-start(f32[2,2,2,128]{3,2,1,0:T(2,128)S(1)} %pad_maximum_fusion.46), channel_id=1, source_target_pairs={{16,0},{17,1},{18,2},{19,3},{20,4},{21,5},{22,6},{23,7},{24,8},{25... | collective-permute-start | bytes 12296 | tf_op jit(solution)/shard_map/ppermute | solution.py:20
  120.3 5.6 %collective-permute-start.20 = (f32[6,2,2,128]{3,2,1,0:T(2,128)S(1)}, f32[6,2,2,128]{3,2,1,0:T(2,128)S(1)}, u32[]{:S(2)}, u32[]{:S(2)}) collective-permute-start(f32[6,2,2,128]{3,2,1,0:T(2,128)S(1)} %fusion.281), channel_id=1, source_target_pairs={{0,4},{4,8},{8,12},{1,5},{5,9},{9,13},{2,6},{6,10},{10,14},{3,7},{... | collective-permute-start | bytes 36872 | tf_op jit(solution)/shard_map/ppermute | solution.py:19
  122.3 5.0 %collective-permute-start.21 = (f32[6,2,2,128]{3,2,1,0:T(2,128)S(1)}, f32[6,2,2,128]{3,2,1,0:T(2,128)S(1)}, u32[]{:S(2)}, u32[]{:S(2)}) collective-permute-start(f32[6,2,2,128]{3,2,1,0:T(2,128)S(1)} %fusion.281), channel_id=1, source_target_pairs={{4,0},{8,4},{12,8},{5,1},{9,5},{13,9},{6,2},{10,6},{14,10},{7,3},{... | collective-permute-start | bytes 36872 | tf_op jit(solution)/shard_map/ppermute | solution.py:20
  128.0 6.0 %collective-permute-start.22 = (f32[6,6,2,128]{3,2,1,0:T(2,128)}, f32[6,6,2,128]{3,2,1,0:T(2,128)S(1)}, u32[]{:S(2)}, u32[]{:S(2)}) collective-permute-start(f32[6,6,2,128]{3,2,1,0:T(2,128)} %fusion.211), channel_id=1, source_target_pairs={{0,1},{1,2},{2,3},{4,5},{5,6},{6,7},{8,9},{9,10},{10,11},{12,13},{... | collective-permute-start | bytes 110600 | tf_op jit(solution)/shard_map/ppermute | solution.py:19
  129.9 6.2 %collective-permute-start.23 = (f32[6,6,2,128]{3,2,1,0:T(2,128)}, f32[6,6,2,128]{3,2,1,0:T(2,128)}, u32[]{:S(2)}, u32[]{:S(2)}) collective-permute-start(f32[6,6,2,128]{3,2,1,0:T(2,128)} %fusion.211), channel_id=1, source_target_pairs={{1,0},{2,1},{3,2},{5,4},{6,5},{7,6},{9,8},{10,9},{11,10},{13,12},{... | collective-permute-start | bytes 110600 | tf_op jit(solution)/shard_map/ppermute | solution.py:20
  182.0 5.8 %collective-permute-start.24 = (f32[2,2,2,128]{3,2,1,0:T(2,128)S(1)}, f32[2,2,2,128]{3,2,1,0:T(2,128)S(1)}, u32[]{:S(2)}, u32[]{:S(2)}) collective-permute-start(f32[2,2,2,128]{3,2,1,0:T(2,128)S(1)} %pad_maximum_fusion.47), channel_id=1, source_target_pairs={{0,16},{1,17},{2,18},{3,19},{4,20},{5,21},{6,22},{7,23},{8,24},{9,... | collective-permute-start | bytes 12296 | tf_op jit(solution)/shard_map/ppermute | solution.py:19
  183.3 5.9 %collective-permute-start.25 = (f32[2,2,2,128]{3,2,1,0:T(2,128)S(1)}, f32[2,2,2,128]{3,2,1,0:T(2,128)S(1)}, u32[]{:S(2)}, u32[]{:S(2)}) collective-permute-start(f32[2,2,2,128]{3,2,1,0:T(2,128)S(1)} %pad_maximum_fusion.47), channel_id=1, source_target_pairs={{16,0},{17,1},{18,2},{19,3},{20,4},{21,5},{22,6},{23,7},{24,8},{25... | collective-permute-start | bytes 12296 | tf_op jit(solution)/shard_map/ppermute | solution.py:20
  189.2 5.6 %collective-permute-start.26 = (f32[6,2,2,128]{3,2,1,0:T(2,128)S(1)}, f32[6,2,2,128]{3,2,1,0:T(2,128)S(1)}, u32[]{:S(2)}, u32[]{:S(2)}) collective-permute-start(f32[6,2,2,128]{3,2,1,0:T(2,128)S(1)} %fusion.283), channel_id=1, source_target_pairs={{0,4},{4,8},{8,12},{1,5},{5,9},{9,13},{2,6},{6,10},{10,14},{3,7},{... | collective-permute-start | bytes 36872 | tf_op jit(solution)/shard_map/ppermute | solution.py:19
  191.2 5.0 %collective-permute-start.27 = (f32[6,2,2,128]{3,2,1,0:T(2,128)S(1)}, f32[6,2,2,128]{3,2,1,0:T(2,128)S(1)}, u32[]{:S(2)}, u32[]{:S(2)}) collective-permute-start(f32[6,2,2,128]{3,2,1,0:T(2,128)S(1)} %fusion.283), channel_id=1, source_target_pairs={{4,0},{8,4},{12,8},{5,1},{9,5},{13,9},{6,2},{10,6},{14,10},{7,3},{... | collective-permute-start | bytes 36872 | tf_op jit(solution)/shard_map/ppermute | solution.py:20
  196.3 5.8 %collective-permute-start.28 = (f32[6,6,2,128]{3,2,1,0:T(2,128)S(1)}, f32[6,6,2,128]{3,2,1,0:T(2,128)S(1)}, u32[]{:S(2)}, u32[]{:S(2)}) collective-permute-start(f32[6,6,2,128]{3,2,1,0:T(2,128)S(1)} %fusion.215), channel_id=1, source_target_pairs={{0,1},{1,2},{2,3},{4,5},{5,6},{6,7},{8,9},{9,10},{10,11},{12,13},{... | collective-permute-start | bytes 110600 | tf_op jit(solution)/shard_map/ppermute | solution.py:19
  198.8 5.9 %collective-permute-start.29 = (f32[6,6,2,128]{3,2,1,0:T(2,128)S(1)}, f32[6,6,2,128]{3,2,1,0:T(2,128)S(1)}, u32[]{:S(2)}, u32[]{:S(2)}) collective-permute-start(f32[6,6,2,128]{3,2,1,0:T(2,128)S(1)} %fusion.215), channel_id=1, source_target_pairs={{1,0},{2,1},{3,2},{5,4},{6,5},{7,6},{9,8},{10,9},{11,10},{13,12},{... | collective-permute-start | bytes 110600 | tf_op jit(solution)/shard_map/ppermute | solution.py:20
  205.1 5.9 %collective-permute-start.30 = (f32[2,4,4,128]{3,2,1,0:T(4,128)S(1)}, f32[2,4,4,128]{3,2,1,0:T(4,128)S(1)}, u32[]{:S(2)}, u32[]{:S(2)}) collective-permute-start(f32[2,4,4,128]{3,2,1,0:T(4,128)S(1)} %get-tuple-element.42), channel_id=1, source_target_pairs={{0,16},{1,17},{2,18},{3,19},{4,20},{5,21},{6,22},{7,23},{8,24},{9,... | collective-permute-start | bytes 49160 | tf_op jit(solution)/shard_map/ppermute | solution.py:19
  206.4 6.0 %collective-permute-start.31 = (f32[2,4,4,128]{3,2,1,0:T(4,128)S(1)}, f32[2,4,4,128]{3,2,1,0:T(4,128)S(1)}, u32[]{:S(2)}, u32[]{:S(2)}) collective-permute-start(f32[2,4,4,128]{3,2,1,0:T(4,128)S(1)} %get-tuple-element.43), channel_id=1, source_target_pairs={{16,0},{17,1},{18,2},{19,3},{20,4},{21,5},{22,6},{23,7},{24,8},{25... | collective-permute-start | bytes 49160 | tf_op jit(solution)/shard_map/ppermute | solution.py:20
  212.5 5.6 %collective-permute-start.32 = (f32[8,2,4,128]{3,2,1,0:T(4,128)S(1)}, f32[8,2,4,128]{3,2,1,0:T(4,128)S(1)}, u32[]{:S(2)}, u32[]{:S(2)}) collective-permute-start(f32[8,2,4,128]{3,2,1,0:T(4,128)S(1)} %get-tuple-element.40), channel_id=1, source_target_pairs={{0,4},{4,8},{8,12},{1,5},{5,9},{9,13},{2,6},{6,10},{10,14},{3,7},{... | collective-permute-start | bytes 98312 | tf_op jit(solution)/shard_map/ppermute | solution.py:19
  214.4 5.2 %collective-permute-start.33 = (f32[8,2,4,128]{3,2,1,0:T(4,128)S(1)}, f32[8,2,4,128]{3,2,1,0:T(4,128)S(1)}, u32[]{:S(2)}, u32[]{:S(2)}) collective-permute-start(f32[8,2,4,128]{3,2,1,0:T(4,128)S(1)} %get-tuple-element.41), channel_id=1, source_target_pairs={{4,0},{8,4},{12,8},{5,1},{9,5},{13,9},{6,2},{10,6},{14,10},{7,3},{... | collective-permute-start | bytes 98312 | tf_op jit(solution)/shard_map/ppermute | solution.py:20
  219.8 6.2 %collective-permute-start.34 = (f32[8,8,2,128]{3,2,1,0:T(2,128)S(1)}, f32[8,8,2,128]{3,2,1,0:T(2,128)S(1)}, u32[]{:S(2)}, u32[]{:S(2)}) collective-permute-start(f32[8,8,2,128]{3,2,1,0:T(2,128)S(1)} %get-tuple-element.37), channel_id=1, source_target_pairs={{0,1},{1,2},{2,3},{4,5},{5,6},{6,7},{8,9},{9,10},{10,11},{12,13},{... | collective-permute-start | bytes 196616 | tf_op jit(solution)/shard_map/ppermute | solution.py:19
  221.7 6.2 %collective-permute-start.35 = (f32[8,8,2,128]{3,2,1,0:T(2,128)S(1)}, f32[8,8,2,128]{3,2,1,0:T(2,128)S(1)}, u32[]{:S(2)}, u32[]{:S(2)}) collective-permute-start(f32[8,8,2,128]{3,2,1,0:T(2,128)S(1)} %get-tuple-element.36), channel_id=1, source_target_pairs={{1,0},{2,1},{3,2},{5,4},{6,5},{7,6},{9,8},{10,9},{11,10},{13,12},{... | collective-permute-start | bytes 196616 | tf_op jit(solution)/shard_map/ppermute | solution.py:20
  229.2 6.2 %collective-permute-start.36 = (f32[2,8,8,128]{3,2,1,0:T(8,128)S(1)}, f32[2,8,8,128]{3,2,1,0:T(8,128)S(1)}, u32[]{:S(2)}, u32[]{:S(2)}) collective-permute-start(f32[2,8,8,128]{3,2,1,0:T(8,128)S(1)} %get-tuple-element.31), channel_id=1, source_target_pairs={{0,16},{1,17},{2,18},{3,19},{4,20},{5,21},{6,22},{7,23},{8,24},{9,... | collective-permute-start | bytes 196616 | tf_op jit(solution)/shard_map/ppermute | solution.py:19
  230.5 6.4 %collective-permute-start.37 = (f32[2,8,8,128]{3,2,1,0:T(8,128)S(1)}, f32[2,8,8,128]{3,2,1,0:T(8,128)S(1)}, u32[]{:S(2)}, u32[]{:S(2)}) collective-permute-start(f32[2,8,8,128]{3,2,1,0:T(8,128)S(1)} %get-tuple-element.32), channel_id=1, source_target_pairs={{16,0},{17,1},{18,2},{19,3},{20,4},{21,5},{22,6},{23,7},{24,8},{25... | collective-permute-start | bytes 196616 | tf_op jit(solution)/shard_map/ppermute | solution.py:20
  237.2 5.9 %collective-permute-start.38 = (f32[12,2,8,128]{3,2,1,0:T(8,128)S(1)}, f32[12,2,8,128]{3,2,1,0:T(8,128)S(1)}, u32[]{:S(2)}, u32[]{:S(2)}) collective-permute-start(f32[12,2,8,128]{3,2,1,0:T(8,128)S(1)} %get-tuple-element.27), channel_id=1, source_target_pairs={{0,4},{4,8},{8,12},{1,5},{5,9},{9,13},{2,6},{6,10},{10,14},{3,7},{... | collective-permute-start | bytes 294920 | tf_op jit(solution)/shard_map/ppermute | solution.py:19
  239.1 5.8 %collective-permute-start.39 = (f32[12,2,8,128]{3,2,1,0:T(8,128)S(1)}, f32[12,2,8,128]{3,2,1,0:T(8,128)S(1)}, u32[]{:S(2)}, u32[]{:S(2)}) collective-permute-start(f32[12,2,8,128]{3,2,1,0:T(8,128)S(1)} %get-tuple-element.28), channel_id=1, source_target_pairs={{4,0},{8,4},{12,8},{5,1},{9,5},{13,9},{6,2},{10,6},{14,10},{7,3},{... | collective-permute-start | bytes 294920 | tf_op jit(solution)/shard_map/ppermute | solution.py:20
  245.2 7.0 %collective-permute-start.40 = (f32[12,12,2,128]{3,2,1,0:T(2,128)S(1)}, f32[12,12,2,128]{3,2,1,0:T(2,128)S(1)}, u32[]{:S(2)}, u32[]{:S(2)}) collective-permute-start(f32[12,12,2,128]{3,2,1,0:T(2,128)S(1)} %get-tuple-element.24), channel_id=1, source_target_pairs={{0,1},{1,2},{2,3},{4,5},{5,6},{6,7},{8,9},{9,10},{10,11},{12,13},{... | collective-permute-start | bytes 442376 | tf_op jit(solution)/shard_map/ppermute | solution.py:19
  247.1 7.0 %collective-permute-start.41 = (f32[12,12,2,128]{3,2,1,0:T(2,128)S(1)}, f32[12,12,2,128]{3,2,1,0:T(2,128)S(1)}, u32[]{:S(2)}, u32[]{:S(2)}) collective-permute-start(f32[12,12,2,128]{3,2,1,0:T(2,128)S(1)} %get-tuple-element.23), channel_id=1, source_target_pairs={{1,0},{2,1},{3,2},{5,4},{6,5},{7,6},{9,8},{10,9},{11,10},{13,12},{... | collective-permute-start | bytes 442376 | tf_op jit(solution)/shard_map/ppermute | solution.py:20
  258.8 8.3 %collective-permute-start.42 = (f32[2,16,16,128]{3,2,1,0:T(8,128)S(1)}, f32[2,16,16,128]{3,2,1,0:T(8,128)S(1)}, u32[]{:S(2)}, u32[]{:S(2)}) collective-permute-start(f32[2,16,16,128]{3,2,1,0:T(8,128)S(1)} %get-tuple-element.20), channel_id=1, source_target_pairs={{0,16},{1,17},{2,18},{3,19},{4,20},{5,21},{6,22},{7,23},{8,24},{9,... | collective-permute-start | bytes 786440 | tf_op jit(solution)/shard_map/ppermute | solution.py:19
  260.1 8.4 %collective-permute-start.43 = (f32[2,16,16,128]{3,2,1,0:T(8,128)S(1)}, f32[2,16,16,128]{3,2,1,0:T(8,128)S(1)}, u32[]{:S(2)}, u32[]{:S(2)}) collective-permute-start(f32[2,16,16,128]{3,2,1,0:T(8,128)S(1)} %get-tuple-element.21), channel_id=1, source_target_pairs={{16,0},{17,1},{18,2},{19,3},{20,4},{21,5},{22,6},{23,7},{24,8},{25... | collective-permute-start | bytes 786440 | tf_op jit(solution)/shard_map/ppermute | solution.py:20
  269.2 8.4 %collective-permute-start.44 = (f32[20,2,16,128]{3,2,1,0:T(8,128)S(1)}, f32[20,2,16,128]{3,2,1,0:T(8,128)S(1)}, u32[]{:S(2)}, u32[]{:S(2)}) collective-permute-start(f32[20,2,16,128]{3,2,1,0:T(8,128)S(1)} %get-tuple-element.16), channel_id=1, source_target_pairs={{0,4},{4,8},{8,12},{1,5},{5,9},{9,13},{2,6},{6,10},{10,14},{3,7},{... | collective-permute-start | bytes 983048 | tf_op jit(solution)/shard_map/ppermute | solution.py:19
  271.2 8.2 %collective-permute-start.45 = (f32[20,2,16,128]{3,2,1,0:T(8,128)S(1)}, f32[20,2,16,128]{3,2,1,0:T(8,128)S(1)}, u32[]{:S(2)}, u32[]{:S(2)}) collective-permute-start(f32[20,2,16,128]{3,2,1,0:T(8,128)S(1)} %get-tuple-element.17), channel_id=1, source_target_pairs={{4,0},{8,4},{12,8},{5,1},{9,5},{13,9},{6,2},{10,6},{14,10},{7,3},{... | collective-permute-start | bytes 983048 | tf_op jit(solution)/shard_map/ppermute | solution.py:20
  281.3 10.2 %collective-permute-start.46 = (f32[20,20,2,128]{3,2,1,0:T(2,128)}, f32[20,20,2,128]{3,2,1,0:T(2,128)}, u32[]{:S(2)}, u32[]{:S(2)}) collective-permute-start(f32[20,20,2,128]{3,2,1,0:T(2,128)} %get-tuple-element.13), channel_id=1, source_target_pairs={{0,1},{1,2},{2,3},{4,5},{5,6},{6,7},{8,9},{9,10},{10,11},{12,13},{... | collective-permute-start | bytes 1228808 | tf_op jit(solution)/shard_map/ppermute | solution.py:19
  283.2 10.4 %collective-permute-start.47 = (f32[20,20,2,128]{3,2,1,0:T(2,128)}, f32[20,20,2,128]{3,2,1,0:T(2,128)}, u32[]{:S(2)}, u32[]{:S(2)}) collective-permute-start(f32[20,20,2,128]{3,2,1,0:T(2,128)} %get-tuple-element.12), channel_id=1, source_target_pairs={{1,0},{2,1},{3,2},{5,4},{6,5},{7,6},{9,8},{10,9},{11,10},{13,12},{... | collective-permute-start | bytes 1228808 | tf_op jit(solution)/shard_map/ppermute | solution.py:20
  (19 other events, 295.5 us)
